TPU v7x, 128 devices: a whole 4x4x4 slice. The times are simulated.
128 devices in a mesh: grp: 4 (over z), dev: 32 (over y, x, core).
Axes of the slice: x: 4, y: 4, z: 4, core: 2. Of those that a mesh axis runs over, the one named last changes fastest.
Arguments:
- old_state: float32 [32768, 4, 512], P(('grp', 'dev')), may hold values from -6 to 6
- dest_row: int32 [32768], P(('grp', 'dev')), may hold values from -1 to 16383, as said below
- neighbours: int32 [6, 16384], P(None, ('grp', 'dev')), may hold values from 0 to 16383, as said below
- orientation: int32 [6, 16384], P(None, ('grp', 'dev')), may hold values from 0 to 7
- wall_flags: int32 [6, 16384], P(None, ('grp', 'dev')), may hold values from 0 to 1, as said below
- bulk_modulus: float32 [16384], P(('grp', 'dev')), may hold values from 0.5 to 2
- density: float32 [16384], P(('grp', 'dev')), may hold values from 0.5 to 2
Outputs:
- tendency: float32 [16384, 4, 512], P(('grp', 'dev'))
Inputs may be any that keep to these rules, and one draw needn't show every extreme that they name: `dest_row`: each of the 16384 new rows appears exactly once. On half of the devices every slot is used, on the others every slot is -1. The slots of one device whose new rows lie on one device number either 0 or 8. The elements form a grid of 16 x 32 x 32 cubes along x, y, z, cut into blocks of 4 x 4 x 8, faces 0 to 5 looking to -x, +x, -y, +y, -z, +z; a face on the grid's outside has the row itself as neighbour. If neighbours[f, r] = m differs from r then neighbours[f xor 1, m] = r. Each device holds the rows of one whole block, in rows 128 * i to 128 * (i + 1) - 1 for device index i = g * 32 + d (g of grp, d of dev); which block lies on which device is arbitrary. One device's rows and faces have at most 32 neighbours on any one other device. wall_flags[f, r] is 1 exactly where neighbours[f, r] = r.
All inputs are finite; a program needn't handle non-finite values.
Results may differ from a plain program's by a relative error of at most 0.0001.
Values sent between devices are 32-bit elements; how exact they have to be, the bound alone decides.
A program may use at most 128 MiB of HBM per device.

v0:
```python
import jax
import jax.numpy as jnp
import numpy as np
from jax import lax
from jax.sharding import PartitionSpec as P

NP = 8
PIECES = 16
HCAP = 32


metric_scale = 0.25


def gll_tables(poly_order):
    num_points = poly_order + 1
    points = -np.cos(np.pi * np.arange(num_points) / poly_order)
    legendre = np.zeros((num_points, num_points))
    for sweeps in range(101):
        legendre[:, 0] = 1.0
        legendre[:, 1] = points
        for degree in range(2, num_points):
            legendre[:, degree] = (
                (2 * degree - 1) * points * legendre[:, degree - 1]
                - (degree - 1) * legendre[:, degree - 2]
            ) / degree
        if sweeps < 100:
            points = points - (points * legendre[:, poly_order] - legendre[:, poly_order - 1]) / (
                num_points * legendre[:, poly_order]
            )
    end_values = legendre[:, poly_order]
    weights = 2.0 / (poly_order * num_points * end_values**2)
    distance = points[:, None] - points[None, :] + np.eye(num_points)
    derivative = end_values[:, None] / end_values[None, :] / distance
    derivative = derivative * (1.0 - np.eye(num_points))
    derivative[0, 0] = -poly_order * num_points / 4.0
    derivative[poly_order, poly_order] = poly_order * num_points / 4.0
    return (points, weights, derivative)


def face_index(face_id):
    picked = [slice(None), slice(None), slice(None)]
    picked[face_id // 2] = 0 if face_id % 2 == 0 else NP - 1
    return tuple(picked)


def face_traces(volume):
    return jnp.stack(
        [volume[(slice(None), slice(None)) + face_index(face_id)] for face_id in range(6)]
    )


def orient_trace(values, orient_code):
    shaped = orient_code[:, None, None, None]
    values = jnp.where(shaped % 2 == 1, values[:, :, ::-1, :], values)
    values = jnp.where(shaped // 2 % 2 == 1, values[:, :, :, ::-1], values)
    return jnp.where(shaped >= 4, jnp.swapaxes(values, 2, 3), values)


def derivative_along(scalar_field, matrix, axis_id):
    einsum_forms = ["ai,eijk->eajk", "aj,eijk->eiak", "ak,eijk->eija"]
    return jnp.einsum(einsum_forms[axis_id], matrix, scalar_field, precision=lax.Precision.HIGHEST)


def right_side(
    volume,
    inner_faces,
    outer_faces,
    outer_impedance,
    orientation,
    wall_flags,
    bulk_modulus,
    density,
):
    points, weights, derivative = gll_tables(NP - 1)
    matrix = jnp.asarray(derivative, jnp.float32)
    lift_factor = metric_scale / float(weights[0])
    bulk_vol = bulk_modulus[:, None, None, None]
    dens_vol = density[:, None, None, None]
    divergence = (
        derivative_along(volume[:, 1], matrix, 0)
        + derivative_along(volume[:, 2], matrix, 1)
        + derivative_along(volume[:, 3], matrix, 2)
    )
    pieces_list = [-metric_scale * bulk_vol * divergence]
    for axis_id in range(3):
        pieces_list.append(
            -(metric_scale / dens_vol) * derivative_along(volume[:, 0], matrix, axis_id)
        )
    result = jnp.stack(pieces_list, axis=1)
    inner_impedance = jnp.sqrt(bulk_modulus * density)
    for face_id in range(6):
        axis_id = face_id // 2
        normal_sign = 2.0 * (face_id % 2) - 1.0
        own_face = inner_faces[face_id]
        far_face = orient_trace(outer_faces[face_id], orientation[face_id])
        is_wall = wall_flags[face_id] == 1
        wall_face = is_wall[:, None, None]
        press_in = own_face[:, 0]
        normal_in = normal_sign * own_face[:, 1 + axis_id]
        press_out = jnp.where(wall_face, press_in, far_face[:, 0])
        normal_out = jnp.where(wall_face, -normal_in, normal_sign * far_face[:, 1 + axis_id])
        imped_in = inner_impedance[:, None, None]
        imped_out = jnp.where(is_wall, inner_impedance, outer_impedance[face_id])[:, None, None]
        imped_sum = imped_in + imped_out
        press_star = (
            imped_out * press_in
            + imped_in * press_out
            + imped_in * imped_out * (normal_in - normal_out)
        ) / imped_sum
        normal_star = (
            imped_in * normal_in + imped_out * normal_out + press_in - press_out
        ) / imped_sum
        result = result.at[(slice(None), 0) + face_index(face_id)].add(
            -lift_factor * bulk_modulus[:, None, None] * (normal_star - normal_in)
        )
        result = result.at[(slice(None), 1 + axis_id) + face_index(face_id)].add(
            -(normal_sign * lift_factor) * (press_star - press_in) / density[:, None, None]
        )
    return result.reshape(result.shape[0], 4, -1)


def body(old_state, dest_row, neighbours, orientation, wall_flags, bulk_modulus, density):
    elem_dev = bulk_modulus.shape[0]
    groups = lax.axis_size("grp")
    members = lax.axis_size("dev")
    devices = groups * members
    per_pair = elem_dev // PIECES
    is_used = dest_row >= 0
    dest_dev = jnp.where(is_used, dest_row // elem_dev, -1)
    match_grid = (dest_dev[:, None] == jnp.arange(devices)[None, :]).astype(jnp.int32)
    before = jnp.cumsum(match_grid, axis=0) - match_grid
    within = jnp.sum(before * match_grid, axis=1)
    slot_at = jnp.where(is_used, dest_dev * per_pair + within, devices * per_pair)
    outgoing = (
        jnp.zeros((devices * per_pair, 4, old_state.shape[2]), jnp.float32)
        .at[slot_at]
        .set(old_state, mode="drop")
    )
    labels = (
        jnp.zeros((devices * per_pair,), jnp.int32)
        .at[slot_at]
        .set(dest_row % elem_dev + 1, mode="drop")
    )
    arrived, arrived_lab = (
        lax.all_to_all(outgoing, ("grp", "dev"), split_axis=0, concat_axis=0, tiled=True),
        lax.all_to_all(labels, ("grp", "dev"), split_axis=0, concat_axis=0, tiled=True),
    )
    place_at = jnp.where(arrived_lab > 0, arrived_lab - 1, elem_dev)
    new_state = (
        jnp.zeros((elem_dev, 4, old_state.shape[2]), jnp.float32)
        .at[place_at]
        .set(arrived, mode="drop")
    )
    volume = new_state.reshape(elem_dev, 4, NP, NP, NP)
    inner_faces = face_traces(volume)
    flat_inner = inner_faces.reshape(6, elem_dev, 4 * NP * NP)
    face_width = flat_inner.shape[2]
    impedance = jnp.sqrt(bulk_modulus * density)
    my_index = lax.axis_index("grp") * members + lax.axis_index("dev")
    owner_dev = neighbours // elem_dev
    local_row = neighbours - owner_dev * elem_dev
    remote = (owner_dev != my_index) & (wall_flags == 0)
    near_row = jnp.where(remote, 0, local_row)
    outer_faces = jnp.stack([flat_inner[face_id ^ 1][near_row[face_id]] for face_id in range(6)])
    outer_impedance = impedance[near_row]
    slot_count = HCAP
    remote_flat = remote.reshape(-1)
    owner_flat = owner_dev.reshape(-1)
    match_owner = (
        (owner_flat[:, None] == jnp.arange(devices)[None, :]) & remote_flat[:, None]
    ).astype(jnp.int32)
    owner_before = jnp.cumsum(match_owner, axis=0) - match_owner
    owner_rank = jnp.sum(owner_before * match_owner, axis=1)
    ask_slot = jnp.where(remote_flat, owner_flat * slot_count + owner_rank, devices * slot_count)
    ask_value = ((jnp.arange(6) ^ 1)[:, None] * elem_dev + local_row).reshape(-1) + 1
    requests_out = (
        jnp.zeros((devices * slot_count,), jnp.int32).at[ask_slot].set(ask_value, mode="drop")
    )
    trace_table = flat_inner.reshape(6 * elem_dev, face_width)
    incoming = lax.all_to_all(requests_out, ("grp", "dev"), split_axis=0, concat_axis=0, tiled=True)
    serve_at = jnp.maximum(incoming - 1, 0)
    asked = (incoming > 0).astype(jnp.float32)
    answer = trace_table[serve_at] * asked[:, None]
    answer_imped = impedance[serve_at % elem_dev] * asked
    back_trace, back_imped = (
        lax.all_to_all(answer, ("grp", "dev"), split_axis=0, concat_axis=0, tiled=True),
        lax.all_to_all(answer_imped, ("grp", "dev"), split_axis=0, concat_axis=0, tiled=True),
    )
    take_at = jnp.minimum(ask_slot, devices * slot_count - 1)
    outer_faces = jnp.where(
        remote[:, :, None], back_trace[take_at].reshape(6, elem_dev, face_width), outer_faces
    )
    outer_impedance = jnp.where(remote, back_imped[take_at].reshape(6, elem_dev), outer_impedance)
    outer_shaped = outer_faces.reshape(6, elem_dev, 4, NP, NP)
    return right_side(
        volume,
        inner_faces,
        outer_shaped,
        outer_impedance,
        orientation,
        wall_flags,
        bulk_modulus,
        density,
    )


def solution(mesh):
    in_specs = (
        P(("grp", "dev"), None, None),
        P(("grp", "dev")),
        P(None, ("grp", "dev")),
        P(None, ("grp", "dev")),
        P(None, ("grp", "dev")),
        P(("grp", "dev")),
        P(("grp", "dev")),
    )
    out_specs = P(("grp", "dev"), None, None)
    return jax.shard_map(body, mesh=mesh, in_specs=in_specs, out_specs=out_specs, check_vma=False)
```

profile of v0, /device:TPU:1, one launch (start us, length us, event | category | flops | bytes accessed | tf_op | source)
XLA Modules:
  0.0 374.5 jit_solution(12423309612712494848)
XLA Ops:
  0.0 0.8 add_bitcast_fusion
  1.6 0.4 fusion.10
  2.0 3.4 scatter_custom_fusion.3
  5.4 0.7 all_to_all.30
  6.1 11.5 %all-to-all-start.2 = ((s32[128,32,1]{1,2,0:T(1,128)}), s32[128,32,1]{1,2,0:T(1,128)S(1)}, u32[]{:S(2)}, u32[]{:S(2)}) async-start(s32[128,32,1]{1,2,0:T(1,128)} %bitcast.31), calls=%async_computation.2 | async-start | bytes 131072 | tf_op jit(solution)/shard_map/all_to_all | solution.py:181
  17.6 0.7 fusion.113
  18.3 0.7 fusion.64
  19.7 0.6 broadcast_multiply_fusion.2
  20.2 1.4 scatter_custom_fusion
  21.7 0.7 all_to_all.27
  22.4 4.9 %all-to-all-done.2 = s32[128,32,1]{1,2,0:T(1,128)S(1)} async-done(((s32[128,32,1]{1,2,0:T(1,128)}), s32[128,32,1]{1,2,0:T(1,128)S(1)}, u32[]{:S(2)}, u32[]{:S(2)}) %all-to-all-start.2) | async-done | bytes 16416 | tf_op jit(solution)/shard_map/all_to_all | solution.py:181
  27.3 4.9 %all-to-all-start = ((s32[128,8,1]{1,2,0:T(1,128)}), s32[128,8,1]{1,2,0:T(1,128)S(1)}, u32[]{:S(2)}, u32[]{:S(2)}) async-start(s32[128,8,1]{1,2,0:T(1,128)} %bitcast.4), calls=%async_computation | async-start | bytes 131072 | tf_op jit(solution)/shard_map/all_to_all | solution.py:147
  32.4 24.7 %gather_fusion = f32[4096]{0:T(1024)S(1)} fusion(f32[128]{0:T(128)S(1)} %get-tuple-element.271, s32[4096]{0:T(1024)S(1)} %get-tuple-element.282), kind=kCustom, calls=%fused_computation | custom fusion | bytes 49152 | tf_op jit(solution)/shard_map/gather | solution.py:185
  57.2 0.7 broadcast_select_fusion.12
  57.8 9.8 %all-to-all-start.3 = ((f32[128,32,1]{1,2,0:T(1,128)}), f32[128,32,1]{1,2,0:T(1,128)S(1)}, u32[]{:S(2)}, u32[]{:S(2)}) async-start(f32[128,32,1]{1,2,0:T(1,128)} %bitcast.35), calls=%async_computation.3 | async-start | bytes 131072 | tf_op jit(solution)/shard_map/all_to_all | solution.py:188
  67.6 4.4 %broadcast_in_dim.237 = f32[1024,4,512]{2,1,0:T(4,128)} broadcast(f32[]{:T(128)} %constant.543.clone.1), dimensions={} | broadcast | bytes 8388612 | tf_op jit(solution)/shard_map/broadcast_in_dim | solution.py:136
  72.0 23.7 %scatter_fusion = f32[1024,4,512]{2,1,0:T(4,128)} fusion(f32[1024,4,512]{2,1,0:T(4,128)} %broadcast_in_dim.237, s32[256]{0:T(256)S(1)} %get-tuple-element.259, f32[256,4,512]{2,1,0:T(4,128)S(1)} %copy-done), kind=kCustom, calls=%fused_computation.12 | custom fusion | bytes 6292480 | tf_op jit(solution)/shard_map/scatter | solution.py:138
  95.7 13.1 %all-to-all-start.1 = ((f32[1024,4,512]{2,1,0:T(4,128)}), f32[1024,4,512]{2,1,0:T(4,128)}, u32[]{:S(2)}, u32[]{:S(2)}) async-start(f32[1024,4,512]{2,1,0:T(4,128)} %scatter_fusion), calls=%async_computation.1 | async-start | bytes 16777216 | tf_op jit(solution)/shard_map/all_to_all | solution.py:146
  108.8 0.6 fusion.106
  109.4 1.3 concatenate.34
  110.7 1.3 concatenate.35
  112.1 4.8 %gather_fusion.2 = f32[768]{0:T(1024)S(1)} fusion(f32[128]{0:T(128)S(1)} %get-tuple-element.271, s32[1024]{0:T(1024)S(1)} %pad_clamp_fusion.6), kind=kCustom, calls=%fused_computation.2 | custom fusion | bytes 9216 | tf_op jit(solution)/shard_map/gather | solution.py:166
  116.9 0.6 pad_clamp_fusion.2
  117.5 0.6 pad_clamp_fusion
  118.1 0.7 and_reduce_fusion
  118.9 0.7 and_reduce_fusion.2
  119.6 0.6 fusion.75
  120.2 0.6 fusion.74
  120.8 0.6 fusion.70
  121.4 0.5 fusion.66
  121.9 0.6 compare_bitcast_fusion
  122.9 0.5 broadcast.2028
  123.4 0.8 reduce.53
  124.3 4.5 %gather_fusion.1 = f32[768]{0:T(1024)S(1)} fusion(f32[4096]{0:T(1024)S(1)} %all_to_all.33, s32[1024]{0:T(1024)S(1)} %pad_clamp_fusion.7), kind=kCustom, calls=%fused_computation.1 | custom fusion | bytes 9216 | tf_op jit(solution)/shard_map/gather | solution.py:194
  128.8 79.0 %all-to-all-done.1 = f32[1024,4,512]{2,1,0:T(4,128)} async-done(((f32[1024,4,512]{2,1,0:T(4,128)}), f32[1024,4,512]{2,1,0:T(4,128)}, u32[]{:S(2)}, u32[]{:S(2)}) %all-to-all-start.1) | async-done | bytes 8388640 | tf_op jit(solution)/shard_map/all_to_all | solution.py:146
  208.0 61.6 %scatter_fusion.1 = f32[128,4,512]{2,1,0:T(4,128)S(1)} fusion(f32[128,4,512]{2,1,0:T(4,128)S(1)} %broadcast_in_dim.232, s32[1024]{0:T(1024)S(1)} %bitcast.624, f32[1024,4,512]{2,1,0:T(4,128)} %all-to-all-done.1), kind=kCustom, calls=%fused_computation.13 | custom fusion | bytes 25169920 | tf_op jit(solution)/shard_map/scatter | solution.py:153
  269.5 0.4 copy.306
  270.3 0.5 copy.329
  271.2 16.1 %gather_fusion.3 = f32[4096,256]{1,0:T(8,128)} fusion(f32[768,256]{1,0:T(8,128)S(1)} %copy.330, s32[4096]{0:T(1024)S(1)} %get-tuple-element.281), kind=kCustom, calls=%fused_computation.3 | custom fusion | bytes 8404992 | tf_op jit(solution)/shard_map/gather | solution.py:184
  287.3 3.9 %broadcast_multiply_fusion = f32[128,32,256]{2,1,0:T(8,128)} fusion(f32[128,32,256]{2,1,0:T(8,128)} %bitcast.556, f32[128,32]{1,0:T(8,128)S(1)} %convert_bitcast_fusion), kind=kLoop, calls=%fused_computation.15 | loop fusion | flops 1048576 | bytes 8404992 | tf_op jit(solution)/shard_map/mul | solution.py:184
  291.3 12.1 %all-to-all-start.4 = ((f32[128,32,256]{2,1,0:T(8,128)}), f32[128,32,256]{2,1,0:T(8,128)}, u32[]{:S(2)}, u32[]{:S(2)}) async-start(f32[128,32,256]{2,1,0:T(8,128)} %broadcast_multiply_fusion), calls=%async_computation.4 | async-start | bytes 8388608 | tf_op jit(solution)/shard_map/all_to_all | solution.py:187
  303.4 0.6 fusion.92
  304.1 0.5 copy-done.28
  304.6 0.6 fusion.105
  305.2 0.7 slice_bitcast_fusion.23
  306.2 0.8 slice_bitcast_fusion.21
  307.5 0.5 fusion.2
  308.5 0.8 gather_fusion.5
  309.3 0.8 gather_fusion.6
  310.1 0.9 gather_fusion.7
  311.0 0.9 gather_fusion.8
  311.8 0.9 gather_fusion.9
  312.7 0.9 gather_fusion.10
  314.3 0.5 fusion.14
  314.9 0.4 fusion.4
  315.5 40.5 %all-to-all-done.4 = f32[128,32,256]{2,1,0:T(8,128)} async-done(((f32[128,32,256]{2,1,0:T(8,128)}), f32[128,32,256]{2,1,0:T(8,128)}, u32[]{:S(2)}, u32[]{:S(2)}) %all-to-all-start.4) | async-done | bytes 4194336 | tf_op jit(solution)/shard_map/all_to_all | solution.py:187
  356.0 4.3 %gather_fusion.4 = f32[768,256]{1,0:T(8,128)S(1)} fusion(f32[4096,256]{1,0:T(8,128)} %bitcast.49, s32[1024]{0:T(1024)S(1)} %pad_clamp_fusion.7), kind=kCustom, calls=%fused_computation.4 | custom fusion | bytes 1575936 | tf_op jit(solution)/shard_map/gather | solution.py:192
  362.6 0.7 fusion.49
  363.3 1.9 fusion.29
  365.3 1.3 constant_dynamic-slice_fusion
  366.7 1.9 fusion.31
  369.3 2.0 broadcast_select_fusion.4
  371.4 1.4 scatter-add.56
  373.1 1.4 copy.360
  (247 shorter events, 7.7 us)
Async XLA Ops:
  0.0 19.6 %copy-start.10 = (s32[256]{0:T(256)S(1)}, s32[256]{0:T(256)}, u32[]{:S(2)}) copy-start(s32[256]{0:T(256)} %param.33) | copy-start | bytes 3076
  0.0 19.6 %copy-start.63 = (f32[128]{0:T(128)S(1)}, f32[128]{0:T(128)}, u32[]{:S(2)}) copy-start(f32[128]{0:T(128)} %param.37) | copy-start | bytes 1540
  0.0 19.6 %copy-start.7 = (f32[128]{0:T(128)S(1)}, f32[128]{0:T(128)}, u32[]{:S(2)}) copy-start(f32[128]{0:T(128)} %param.38) | copy-start | bytes 1540
  6.1 21.1 %all-to-all-start.2 = ((s32[128,32,1]{1,2,0:T(1,128)}), s32[128,32,1]{1,2,0:T(1,128)S(1)}, u32[]{:S(2)}, u32[]{:S(2)}) async-start(s32[128,32,1]{1,2,0:T(1,128)} %bitcast.31), calls=%async_computation.2 | async-start | bytes 131072 | tf_op jit(solution)/shard_map/all_to_all | solution.py:181
  20.2 287.8 %copy-start.12 = (f32[128]{0:T(128)}, f32[128]{0:T(128)S(1)}, u32[]{:S(2)}) copy-start(f32[128]{0:T(128)S(1)} %get-tuple-element.272) | copy-start | bytes 1540
  27.3 30.6 %all-to-all-start = ((s32[128,8,1]{1,2,0:T(1,128)}), s32[128,8,1]{1,2,0:T(1,128)S(1)}, u32[]{:S(2)}, u32[]{:S(2)}) async-start(s32[128,8,1]{1,2,0:T(1,128)} %bitcast.4), calls=%async_computation | async-start | bytes 131072 | tf_op jit(solution)/shard_map/all_to_all | solution.py:147
  57.8 37.8 %all-to-all-start.3 = ((f32[128,32,1]{1,2,0:T(1,128)}), f32[128,32,1]{1,2,0:T(1,128)S(1)}, u32[]{:S(2)}, u32[]{:S(2)}) async-start(f32[128,32,1]{1,2,0:T(1,128)} %bitcast.35), calls=%async_computation.3 | async-start | bytes 131072 | tf_op jit(solution)/shard_map/all_to_all | solution.py:188
  67.6 4.4 %copy-start = (f32[256,4,512]{2,1,0:T(4,128)S(1)}, f32[256,4,512]{2,1,0:T(4,128)}, u32[]{:S(2)}) copy-start(f32[256,4,512]{2,1,0:T(4,128)} %param.32) | copy-start | bytes 6291460
  95.7 112.1 %all-to-all-start.1 = ((f32[1024,4,512]{2,1,0:T(4,128)}), f32[1024,4,512]{2,1,0:T(4,128)}, u32[]{:S(2)}, u32[]{:S(2)}) async-start(f32[1024,4,512]{2,1,0:T(4,128)} %scatter_fusion), calls=%async_computation.1 | async-start | bytes 16777216 | tf_op jit(solution)/shard_map/all_to_all | solution.py:146
  108.8 9.4 %copy-start.65 = (s32[5]{0:T(128)S(1)}, s32[5]{0:T(128)}, u32[]{:S(2)}) copy-start(s32[5]{0:T(128)} %constant.567.clone.1) | copy-start | bytes 64
  108.8 9.4 %copy-start.66 = (s32[5]{0:T(128)S(1)}, s32[5]{0:T(128)}, u32[]{:S(2)}) copy-start(s32[5]{0:T(128)} %constant.569.clone.1) | copy-start | bytes 64
  108.8 10.1 %copy-start.64 = (s32[5]{0:T(128)S(1)}, s32[5]{0:T(128)}, u32[]{:S(2)}) copy-start(s32[5]{0:T(128)} %constant.565.clone.1) | copy-start | bytes 64
  108.8 10.8 %copy-start.50 = (s32[6,128]{1,0:T(8,128)S(1)}, s32[6,128]{1,0:T(8,128)}, u32[]{:S(2)}) copy-start(s32[6,128]{1,0:T(8,128)} %param.35) | copy-start | bytes 9220
  108.8 13.1 %copy-start.6 = (s32[6,128]{1,0:T(8,128)S(1)}, s32[6,128]{1,0:T(8,128)}, u32[]{:S(2)}) copy-start(s32[6,128]{1,0:T(8,128)} %param.36) | copy-start | bytes 9220
  291.3 64.7 %all-to-all-start.4 = ((f32[128,32,256]{2,1,0:T(8,128)}), f32[128,32,256]{2,1,0:T(8,128)}, u32[]{:S(2)}, u32[]{:S(2)}) async-start(f32[128,32,256]{2,1,0:T(8,128)} %broadcast_multiply_fusion), calls=%async_computation.4 | async-start | bytes 8388608 | tf_op jit(solution)/shard_map/all_to_all | solution.py:187
  303.4 4.1 %copy-start.5 = (f32[8,8,1,1]{1,0,3,2:T(8,128)S(1)}, f32[8,8,1,1]{1,0,3,2:T(8,128)}, u32[]{:S(2)}) copy-start(f32[8,8,1,1]{1,0,3,2:T(8,128)} %constant.571) | copy-start | bytes 772
  304.0 4.5 %copy-start.20 = (f32[128]{0:T(128)}, f32[128]{0:T(128)S(1)}, u32[]{:S(2)}) copy-start(f32[128]{0:T(128)S(1)} %get-tuple-element.152) | copy-start | bytes 1540
  304.1 4.5 %copy-start.22 = (f32[128]{0:T(128)}, f32[128]{0:T(128)S(1)}, u32[]{:S(2)}) copy-start(f32[128]{0:T(128)S(1)} %get-tuple-element.213) | copy-start | bytes 1540
  304.1 4.5 %copy-start.24 = (f32[128]{0:T(128)}, f32[128]{0:T(128)S(1)}, u32[]{:S(2)}) copy-start(f32[128]{0:T(128)S(1)} %get-tuple-element.215) | copy-start | bytes 1540
  304.1 4.5 %copy-start.26 = (f32[128]{0:T(128)}, f32[128]{0:T(128)S(1)}, u32[]{:S(2)}) copy-start(f32[128]{0:T(128)S(1)} %get-tuple-element.217) | copy-start | bytes 1540
  309.3 4.3 %copy-start.13 = (f32[128]{0:T(128)S(1)}, f32[128]{0:T(128)}, u32[]{:S(2)}) copy-start(f32[128]{0:T(128)} %copy-done.12) | copy-start | bytes 1540
  309.3 5.5 %copy-start.52 = (f32[128]{0:T(128)S(1)}, f32[128]{0:T(128)}, u32[]{:S(2)}) copy-start(f32[128]{0:T(128)} %get-tuple-element.269) | copy-start | bytes 1540
  356.0 4.8 %copy-start.19 = (pred[128]{0:T(512)(128)(4,1)S(1)}, pred[128]{0:T(512)(128)(4,1)}, u32[]{:S(2)}) copy-start(pred[128]{0:T(512)(128)(4,1)} %get-tuple-element.278) | copy-start | bytes 388
  356.0 4.9 %copy-start.43 = (pred[128]{0:T(512)(128)(4,1)S(1)}, pred[128]{0:T(512)(128)(4,1)}, u32[]{:S(2)}) copy-start(pred[128]{0:T(512)(128)(4,1)} %get-tuple-element.153) | copy-start | bytes 388
  360.3 1.5 copy-start.17
  360.3 1.6 copy-start.16
  360.5 1.6 copy-start.15
  360.5 1.7 copy-start.41
  360.6 1.7 copy-start.39
  360.6 1.7 copy-start.54
  360.7 1.6 copy-start.38
  360.8 1.6 copy-start.53
  360.9 1.5 copy-start.4
  360.9 1.5 copy-start.9
  360.9 1.6 copy-start.11
  360.9 1.6 copy-start.31
  360.9 1.6 copy-start.40
  361.0 1.6 copy-start.49
  361.0 1.5 copy-start.8
  361.0 2.2 copy-start.3
  361.0 2.2 copy-start.29
  361.1 2.2 copy-start.37
  361.1 2.2 copy-start.48
  361.2 4.0 %copy-start.2 = (f32[128,4,8,8]{0,3,2,1:T(8,128)S(1)}, f32[128,4,8,8]{0,3,2,1:T(8,128)}, u32[]{:S(2)}) copy-start(f32[128,4,8,8]{0,3,2,1:T(8,128)} %get-tuple-element.183) | copy-start | bytes 393220
  361.2 4.0 %copy-start.27 = (f32[128]{0:T(128)S(1)}, f32[128]{0:T(128)}, u32[]{:S(2)}) copy-start(f32[128]{0:T(128)} %copy-done.26) | copy-start | bytes 1540
  361.2 4.0 %copy-start.36 = (pred[128]{0:T(512)(128)(4,1)S(1)}, pred[128]{0:T(512)(128)(4,1)}, u32[]{:S(2)}) copy-start(pred[128]{0:T(512)(128)(4,1)} %get-tuple-element.224) | copy-start | bytes 388
  361.2 4.0 %copy-start.47 = (f32[128]{0:T(128)S(1)}, f32[128]{0:T(128)}, u32[]{:S(2)}) copy-start(f32[128]{0:T(128)} %get-tuple-element.263) | copy-start | bytes 1540
  361.3 5.3 %copy-start.34 = (pred[128]{0:T(512)(128)(4,1)S(1)}, pred[128]{0:T(512)(128)(4,1)}, u32[]{:S(2)}) copy-start(pred[128]{0:T(512)(128)(4,1)} %get-tuple-element.232) | copy-start | bytes 388
  361.3 5.3 %copy-start.51 = (pred[128]{0:T(512)(128)(4,1)S(1)}, pred[128]{0:T(512)(128)(4,1)}, u32[]{:S(2)}) copy-start(pred[128]{0:T(512)(128)(4,1)} %get-tuple-element.240) | copy-start | bytes 388
  361.4 5.3 %copy-start.1 = (f32[128,4,8,8]{0,3,2,1:T(8,128)S(1)}, f32[128,4,8,8]{0,3,2,1:T(8,128)}, u32[]{:S(2)}) copy-start(f32[128,4,8,8]{0,3,2,1:T(8,128)} %get-tuple-element.182) | copy-start | bytes 393220
  361.4 5.3 %copy-start.25 = (f32[128]{0:T(128)S(1)}, f32[128]{0:T(128)}, u32[]{:S(2)}) copy-start(f32[128]{0:T(128)} %copy-done.24) | copy-start | bytes 1540
  361.4 5.3 %copy-start.35 = (pred[128]{0:T(512)(128)(4,1)S(1)}, pred[128]{0:T(512)(128)(4,1)}, u32[]{:S(2)}) copy-start(pred[128]{0:T(512)(128)(4,1)} %get-tuple-element.223) | copy-start | bytes 388
  361.4 5.3 %copy-start.46 = (f32[128]{0:T(128)S(1)}, f32[128]{0:T(128)}, u32[]{:S(2)}) copy-start(f32[128]{0:T(128)} %get-tuple-element.262) | copy-start | bytes 1540
  361.4 7.2 %copy-start.58 = (f32[128]{0:T(128)S(1)}, f32[128]{0:T(128)}, u32[]{:S(2)}) copy-start(f32[128]{0:T(128)} %get-tuple-element.214) | copy-start | bytes 1540
  361.6 7.2 %copy-start.23 = (f32[128]{0:T(128)S(1)}, f32[128]{0:T(128)}, u32[]{:S(2)}) copy-start(f32[128]{0:T(128)} %copy-done.22) | copy-start | bytes 1540
  361.6 7.2 %copy-start.33 = (pred[128]{0:T(512)(128)(4,1)S(1)}, pred[128]{0:T(512)(128)(4,1)}, u32[]{:S(2)}) copy-start(pred[128]{0:T(512)(128)(4,1)} %get-tuple-element.227) | copy-start | bytes 388
  361.6 7.2 %copy-start.45 = (f32[128]{0:T(128)S(1)}, f32[128]{0:T(128)}, u32[]{:S(2)}) copy-start(f32[128]{0:T(128)} %get-tuple-element.261) | copy-start | bytes 1540
  361.6 7.4 %copy-start.57 = (f32[128]{0:T(128)S(1)}, f32[128]{0:T(128)}, u32[]{:S(2)}) copy-start(f32[128]{0:T(128)} %get-tuple-element.212) | copy-start | bytes 1540
  361.7 3.6 copy-start.61
  361.7 7.7 %copy-start.21 = (f32[128]{0:T(128)S(1)}, f32[128]{0:T(128)}, u32[]{:S(2)}) copy-start(f32[128]{0:T(128)} %copy-done.20) | copy-start | bytes 1540
  361.7 7.7 %copy-start.32 = (pred[128]{0:T(512)(128)(4,1)S(1)}, pred[128]{0:T(512)(128)(4,1)}, u32[]{:S(2)}) copy-start(pred[128]{0:T(512)(128)(4,1)} %get-tuple-element.222) | copy-start | bytes 388
  361.7 7.7 %copy-start.44 = (f32[128]{0:T(128)S(1)}, f32[128]{0:T(128)}, u32[]{:S(2)}) copy-start(f32[128]{0:T(128)} %get-tuple-element.260) | copy-start | bytes 1540
  361.8 11.0 %copy-start.55 = (f32[128]{0:T(128)S(1)}, f32[128]{0:T(128)}, u32[]{:S(2)}) copy-start(f32[128]{0:T(128)} %get-tuple-element.151) | copy-start | bytes 1540
  361.9 3.3 copy-start.62
  (8 other events, 7.4 us)
where the time goes:
time: 378 us; the launch traced here: 374 us
  local copies, waits for them, and re-layouts  170 us (45%)
  waiting for transfers between devices  124 us (33%)
  starting transfers between devices  51.3 us (14%)
  other arithmetic  24.3 us (6%)
    all_to_all x1, waiting for transfers between devices, body(): lax.all_to_all(outgoing, ('grp', 'dev'), split_axis=0, concat_axis=0, til...  79 us
    scatter x2, local copies, waits for them, and re-layouts, body(): new_state = jnp.zeros((elem_dev, 4, old_state.shape[2]), jnp.float32).at[...  62 us
    all_to_all x1, waiting for transfers between devices, body(): lax.all_to_all(answer, ('grp', 'dev'), split_axis=0, concat_axis=0, tiled...  40.5 us
    gather x2, local copies, waits for them, and re-layouts, body(): answer_imped = impedance[serve_at % elem_dev] * asked  24.8 us
    scatter x1, local copies, waits for them, and re-layouts, body(): outgoing = jnp.zeros((devices * per_pair, 4, old_state.shape[2]), jnp.flo...  23.7 us
    gather x1, local copies, waits for them, and re-layouts, body(): answer = trace_table[serve_at] * asked[:, None]  16.1 us
    all_to_all x1, starting transfers between devices, body(): lax.all_to_all(outgoing, ('grp', 'dev'), split_axis=0, concat_axis=0, til...  13.1 us
    all_to_all x1, starting transfers between devices, body(): lax.all_to_all(answer, ('grp', 'dev'), split_axis=0, concat_axis=0, tiled...  12.1 us
  transfers between devices with their start and end apart: 5, of which 3 were waited for; matrix products, arithmetic and copies ran while one was open for 24% of the time, Pallas kernels for 0%

commit v1 on v0

--- a/solution.py
+++ b/solution.py
@@ -1,13 +1,17 @@
+import functools
+
 import jax
 import jax.numpy as jnp
 import numpy as np
 from jax import lax
+from jax.experimental import pallas as pl
+from jax.experimental.pallas import tpu as pltpu
 from jax.sharding import PartitionSpec as P
 
 NP = 8
-PIECES = 16
 HCAP = 32
-
+MESH = pl.DeviceIdType.MESH
+HIGHEST = lax.Precision.HIGHEST
 
 metric_scale = 0.25
 
@@ -120,38 +124,222 @@
     return result.reshape(result.shape[0], 4, -1)
 
 
+def my_place():
+    group = lax.axis_index("grp")
+    member = lax.axis_index("dev")
+    return group, member // 8, (member // 2) % 4, member % 2
+
+
+def chip_at(place, step):
+    z_at, y_at, x_at, _ = place
+    x_to = (x_at + step) % 4
+    y_to = (y_at + step // 4 + step) % 4
+    z_to = (z_at + step // 16 + step // 4 + step) % 4
+    return z_to, y_to * 4 + x_to
+
+
+def permute_kernel(place_ref, state_ref, send_ref, sem):
+    def one(slot, carry):
+        at = place_ref[slot]
+        pltpu.make_async_copy(
+            state_ref.at[slot], send_ref.at[pl.ds((at % 8) * 16, 16), at // 8], sem
+        ).start()
+        return carry
+
+    lax.fori_loop(0, 256, one, 0, unroll=8)
+    pltpu.make_async_copy(state_ref, state_ref, sem).wait()
+
+
+def exchange_kernel(
+    note_ref, send_ref, out_ref, notes, first, second, third, table, index, perm, sems
+):
+    place = my_place()
+    mine = place[0] * 32 + lax.axis_index("dev")
+    core = place[3]
+    barrier = pltpu.get_barrier_semaphore()
+
+    def other(step):
+        group, chip = chip_at(place, step // 2)
+        member = chip * 2 + (core + step) % 2
+        return group, member
+
+    def greet(step, carry):
+        group, member = other(step)
+        pl.semaphore_signal(barrier, inc=1, device_id=(group, member), device_id_type=MESH)
+        return carry
+
+    lax.fori_loop(1, 128, greet, 0)
+    pl.semaphore_wait(barrier, 127)
+
+    def copy(source, target, phase, group, member):
+        pltpu.make_async_remote_copy(
+            src_ref=source,
+            dst_ref=target,
+            send_sem=sems.at[2 * phase],
+            recv_sem=sems.at[2 * phase + 1],
+            device_id=(group, member),
+            device_id_type=MESH,
+        ).start()
+
+    def finish(buffer, rows, which):
+        view = buffer.at[pl.ds(0, rows)]
+        pltpu.make_async_copy(view, view, sems.at[which]).wait()
+
+    def tell(step, carry):
+        group, member = other(step)
+        copy(note_ref.at[pl.ds(group * 32 + member, 1)], notes.at[pl.ds(mine, 1)], 0, group, member)
+        return carry
+
+    lax.fori_loop(1, 128, tell, 0)
+
+    def spread(group, member):
+        copy(send_ref.at[group * 32 + member], first.at[pl.ds(mine * 32, 32)], 1, group, member)
+
+    spread(place[0], lax.axis_index("dev") + 1 - 2 * core)
+    for side in range(2):
+
+        def spread_step(step, carry):
+            group, chip = chip_at(place, step)
+            spread(group, chip * 2 + side)
+            return carry
+
+        lax.fori_loop(1, 64, spread_step, 0)
+    notes[pl.ds(mine, 1)] = note_ref[pl.ds(mine, 1)]
+    first[pl.ds(mine * 32, 32)] = send_ref[mine]
+
+    finish(notes, 127, 1)
+    note = notes.reshape(128, 128)[...]
+    lane = lax.broadcasted_iota(jnp.int32, (128, 128), 1)
+    sub = lax.broadcasted_iota(jnp.int32, (128, 128), 0)
+    lower = (lane < sub).astype(jnp.float32)
+    piece = jnp.zeros((128, 128), jnp.int32)
+    for k in range(32):
+        piece = piece + jnp.where(note[:, 32 + k : 33 + k] == lane, k + 1, 0)
+    valid = piece > 0
+    rank = jnp.dot(lower, valid.astype(jnp.float32), preferred_element_type=jnp.float32)
+    rank = rank.astype(jnp.int32)
+    entry = sub * 32 + piece - 1
+    for j in range(16):
+        table[j : j + 1, :] = jnp.sum(
+            jnp.where(valid & (rank == j), entry, 0), axis=0, keepdims=True
+        )
+    to_scalar = pltpu.make_async_copy(table, index, sems.at[8])
+    to_scalar.start()
+    has = jnp.broadcast_to(note[:, 0:1] > 0, (128, 128))
+    order = jnp.dot(lower, has.astype(jnp.float32), preferred_element_type=jnp.float32)
+    slot = jnp.where(has & (order.astype(jnp.int32) == lane), 1.0, 0.0)[:, :16]
+    rows = []
+    for i in range(8):
+        is_row = (note[:, i : i + 1] - 1 == lane).astype(jnp.float32)
+        rows.append(
+            lax.dot_general(
+                slot, is_row, (((0,), (0,)), ((), ())), preferred_element_type=jnp.float32
+            )
+        )
+    perm[...] = jnp.concatenate(rows, axis=0).T
+    to_scalar.wait()
+
+    finish(first, 127 * 32, 3)
+
+    def pick(target, base, at):
+        for j in range(16):
+            target[pl.ds(base + j, 1)] = first[pl.ds(index[j, at], 1)]
+
+    pick(third, mine * 16, mine)
+
+    def forward(step):
+        group, member = other(step)
+        at = group * 32 + member
+        copy(
+            second.at[pl.ds(at * 16, 16)], third.at[pl.ds(mine * 16, 16)], 2, group, member
+        )
+
+    def pick_step(step, carry):
+        group, member = other(step)
+        at = group * 32 + member
+        pick(second, at * 16, at)
+
+        @pl.when(step > 1)
+        def _():
+            forward(step - 1)
+
+        return carry
+
+    lax.fori_loop(1, 128, pick_step, 0)
+    forward(127)
+    finish(third, 127 * 16, 5)
+
+    arrived = third.reshape(8, 16, 16, 128)
+    for part in range(16):
+        block = arrived[:, part].reshape(128, 128)
+        out_ref[pl.ds(part, 128, stride=16), :] = jnp.dot(
+            perm[...], block, precision=HIGHEST, preferred_element_type=jnp.float32
+        )
+    finish(notes, 127, 0)
+    finish(first, 127 * 32, 2)
+    finish(third, 127 * 16, 4)
+
+
+def move_state(old_state, dest_row):
+    below = dest_row[None, :] < dest_row[:, None]
+    tie = (dest_row[None, :] == dest_row[:, None]) & (
+        jnp.arange(256)[None, :] < jnp.arange(256)[:, None]
+    )
+    position = jnp.sum((below | tie).astype(jnp.int32), axis=1)
+    ordered = jnp.sum(
+        jnp.where(position[:, None] == jnp.arange(256)[None, :], dest_row[:, None], 0), axis=0
+    )
+    pieces = ordered.reshape(32, 8)
+    targets = pieces[:, 0] // 128
+    row_ids = jnp.sum(
+        jnp.where(
+            targets[None, :, None] == jnp.arange(128)[:, None, None], pieces[None] % 128 + 1, 0
+        ),
+        axis=1,
+    )
+    note = jnp.concatenate(
+        [
+            row_ids,
+            jnp.zeros((128, 24), jnp.int32),
+            jnp.broadcast_to(targets[None, :], (128, 32)),
+            jnp.zeros((128, 64), jnp.int32),
+        ],
+        axis=1,
+    )[:, None, :]
+    view = old_state.reshape(256, 4, 4, 128).transpose(0, 2, 1, 3).reshape(256, 16, 1, 128)
+    whole = pl.BlockSpec(memory_space=pltpu.VMEM)
+    sends = pl.pallas_call(
+        permute_kernel,
+        out_shape=jax.ShapeDtypeStruct((128, 32, 1, 128), jnp.float32),
+        in_specs=[pl.BlockSpec(memory_space=pltpu.SMEM), pl.BlockSpec(memory_space=pl.ANY)],
+        out_specs=whole,
+        scratch_shapes=[pltpu.SemaphoreType.DMA],
+    )(position, view)
+    moved = pl.pallas_call(
+        exchange_kernel,
+        out_shape=jax.ShapeDtypeStruct((2048, 128), jnp.float32),
+        in_specs=[whole, whole],
+        out_specs=whole,
+        scratch_shapes=[
+            pltpu.VMEM((128, 1, 128), jnp.int32),
+            pltpu.VMEM((4096, 1, 128), jnp.float32),
+            pltpu.VMEM((2048, 1, 128), jnp.float32),
+            pltpu.VMEM((2048, 1, 128), jnp.float32),
+            pltpu.VMEM((16, 128), jnp.int32),
+            pltpu.SMEM((16, 128), jnp.int32),
+            pltpu.VMEM((128, 128), jnp.float32),
+            pltpu.SemaphoreType.DMA((9,)),
+        ],
+        compiler_params=pltpu.CompilerParams(collective_id=0, has_side_effects=True),
+    )(note, sends)
+    return moved.reshape(128, 4, 4, 128).transpose(0, 2, 1, 3).reshape(128, 4, 512)
+
+
 def body(old_state, dest_row, neighbours, orientation, wall_flags, bulk_modulus, density):
     elem_dev = bulk_modulus.shape[0]
-    groups = lax.axis_size("grp")
     members = lax.axis_size("dev")
-    devices = groups * members
-    per_pair = elem_dev // PIECES
-    is_used = dest_row >= 0
-    dest_dev = jnp.where(is_used, dest_row // elem_dev, -1)
-    match_grid = (dest_dev[:, None] == jnp.arange(devices)[None, :]).astype(jnp.int32)
-    before = jnp.cumsum(match_grid, axis=0) - match_grid
-    within = jnp.sum(before * match_grid, axis=1)
-    slot_at = jnp.where(is_used, dest_dev * per_pair + within, devices * per_pair)
-    outgoing = (
-        jnp.zeros((devices * per_pair, 4, old_state.shape[2]), jnp.float32)
-        .at[slot_at]
-        .set(old_state, mode="drop")
-    )
-    labels = (
-        jnp.zeros((devices * per_pair,), jnp.int32)
-        .at[slot_at]
-        .set(dest_row % elem_dev + 1, mode="drop")
-    )
-    arrived, arrived_lab = (
-        lax.all_to_all(outgoing, ("grp", "dev"), split_axis=0, concat_axis=0, tiled=True),
-        lax.all_to_all(labels, ("grp", "dev"), split_axis=0, concat_axis=0, tiled=True),
-    )
-    place_at = jnp.where(arrived_lab > 0, arrived_lab - 1, elem_dev)
-    new_state = (
-        jnp.zeros((elem_dev, 4, old_state.shape[2]), jnp.float32)
-        .at[place_at]
-        .set(arrived, mode="drop")
-    )
+    devices = 128
+    new_state = move_state(old_state, dest_row)
     volume = new_state.reshape(elem_dev, 4, NP, NP, NP)
     inner_faces = face_traces(volume)
     flat_inner = inner_faces.reshape(6, elem_dev, 4 * NP * NP)

time: 378 us -> 233 us (0.62)
  waiting for transfers between devices: 124 us -> 26.7 us
  local copies, waits for them, and re-layouts: 170 us -> 85 us
  Pallas kernels: 0 us -> 65.5 us
  starting transfers between devices: 51.3 us -> 26.1 us
    scatter x4 -> x0, local copies, waits for them, and re-layouts: 87.1 us -> none  [the longest x2 62 us: body(): new_state = jnp.zeros((elem_dev, 4, old_state.shape[2]), jnp.float32).at[...]
    all_to_all x2 -> x0, waiting for transfers between devices: 79.1 us -> none  [the longest x1 79 us: body(): lax.all_to_all(outgoing, ('grp', 'dev'), split_axis=0, concat_axis=0, til...]
    pallas_call x0 -> x2, Pallas kernels: none -> 65.5 us  [the longest x1 60.6 us: move_state(): pl.pallas_call(exchange_kernel, out_shape=jax.ShapeDtypeStruct((2048, 128...]
    all_to_all x2 -> x0, starting transfers between devices: 17.9 us -> none  [the longest x1 13.1 us: body(): lax.all_to_all(outgoing, ('grp', 'dev'), split_axis=0, concat_axis=0, til...]
    all_to_all x1, waiting for transfers between devices: 40.5 us -> 26.7 us  [body(): lax.all_to_all(answer, ('grp', 'dev'), split_axis=0, concat_axis=0, tiled...]
    all_to_all x1, starting transfers between devices: 9.76 us -> 4.43 us  [body(): lax.all_to_all(answer_imped, ('grp', 'dev'), split_axis=0, concat_axis=0,...]
    all_to_all x1, waiting for transfers between devices: 4.9 us -> 0.01 us  [body(): lax.all_to_all(requests_out, ('grp', 'dev'), split_axis=0, concat_axis=0,...]
    broadcast_in_dim x2, local copies, waits for them, and re-layouts: 4.51 us -> 0.01 us  [the longest x1 0.01 us: move_state(): jnp.zeros((128, 24), jnp.int32)]
  transfers between devices with their start and end apart: 5 -> 3, of which waited for: 3 -> 1; matrix products, arithmetic and copies ran while one was open for 24% -> 28% of each run, Pallas kernels for 0% -> 28%
where the time goes in v1:
time: 233 us; the launch traced here: 232 us
  local copies, waits for them, and re-layouts  85 us (36%)
  Pallas kernels  65.5 us (28%)
  waiting for transfers between devices  26.7 us (11%)
  starting transfers between devices  26.1 us (11%)
  other arithmetic  21.8 us (9%)
  matrix products  5.26 us (2%)
    pallas_call x1, Pallas kernels, move_state(): pl.pallas_call(exchange_kernel, out_shape=jax.ShapeDtypeStruct((2048, 128...  60.6 us
    all_to_all x1, waiting for transfers between devices, body(): lax.all_to_all(answer, ('grp', 'dev'), split_axis=0, concat_axis=0, tiled...  26.7 us
    gather x2, local copies, waits for them, and re-layouts, body(): answer_imped = impedance[serve_at % elem_dev] * asked  24.8 us
    gather x1, local copies, waits for them, and re-layouts, body(): answer = trace_table[serve_at] * asked[:, None]  16.2 us
    all_to_all x1, starting transfers between devices, body(): lax.all_to_all(requests_out, ('grp', 'dev'), split_axis=0, concat_axis=0,...  11.5 us
    all_to_all x1, starting transfers between devices, body(): lax.all_to_all(answer, ('grp', 'dev'), split_axis=0, concat_axis=0, tiled...  10.2 us
    gather x6, local copies, waits for them, and re-layouts, body(): flat_inner[face_id ^ 1][near_row[face_id]]  9.15 us
    gather x1, local copies, waits for them, and re-layouts, body(): outer_impedance = impedance[near_row]  6.48 us
  transfers between devices with their start and end apart: 3, of which 1 were waited for; matrix products, arithmetic and copies ran while one was open for 28% of the time, Pallas kernels for 28%

profile of v1, /device:TPU:1, one launch (start us, length us, event | category | flops | bytes accessed | tf_op | source)
XLA Modules:
  0.0 231.7 jit_solution(17913133242113099225)
XLA Ops:
  0.0 0.8 add_bitcast_fusion
  1.0 0.3 fusion.5
  1.5 0.4 fusion.10
  2.0 3.4 %scatter_custom_fusion = s32[4096]{0:T(1024)S(1)} fusion(s32[768]{0:T(1024)S(1)} %get-tuple-element.150, s32[768]{0:T(1024)S(1)} %get-tuple-element.251, s32[]{:T(128)} %constant.530.clone.1), kind=kCustom, calls=%fused_computation.171 | custom fusion | bytes 16388 | tf_op jit(solution)/shard_map/scatter | solution.py:366
  5.4 0.7 all_to_all.18
  6.1 11.5 %all-to-all-start = ((s32[128,32,1]{1,2,0:T(1,128)}), s32[128,32,1]{1,2,0:T(1,128)S(1)}, u32[]{:S(2)}, u32[]{:S(2)}) async-start(s32[128,32,1]{1,2,0:T(1,128)} %bitcast.32), calls=%async_computation | async-start | bytes 131072 | tf_op jit(solution)/shard_map/all_to_all | solution.py:369
  17.6 0.9 convert_reduce_fusion.place_ref
  18.5 0.8 select_reduce_fusion
  20.1 4.9 %shard_map.82.send_ref = f32[128,32,1,128]{3,2,1,0:T(1,128)} custom-call(s32[256]{0:T(256)} %copy-done.24, f32[256,16,1,128]{3,2,1,0:T(1,128)} %bitcast.564), custom_call_target="tpu_custom_call" | custom-call | tf_op jit(solution)/shard_map/pallas_call | solution.py:311
  25.0 0.7 add_add_fusion
  25.7 60.6 %shard_map.83 = f32[2048,128]{1,0:T(8,128)} custom-call(s32[128,1,128]{2,1,0:T(1,128)} %bitcast.611, f32[128,32,1,128]{3,2,1,0:T(1,128)} %shard_map.82.send_ref), custom_call_target="tpu_custom_call" | custom-call | tf_op jit(solution)/shard_map/pallas_call | solution.py:318
  86.4 1.6 copy.392
  88.0 0.2 fusion.92
  88.2 0.8 slice_bitcast_fusion.22
  89.1 0.8 slice_bitcast_fusion.20
  90.0 0.6 fusion.100
  90.6 1.3 concatenate.38
  91.9 1.3 concatenate.39
  93.2 0.5 broadcast_multiply_fusion.2
  93.8 1.1 fusion.13
  94.9 1.0 fusion
  95.9 0.5 fusion.2
  96.5 1.1 fusion.1
  97.6 0.7 and_reduce_fusion.2
  98.3 0.6 pad_clamp_fusion.4
  98.9 0.6 pad_clamp_fusion.2
  99.5 0.6 pad_clamp_fusion
  100.1 0.7 and_reduce_fusion
  100.8 0.5 copy.415
  101.3 0.2 copy.485
  101.4 0.3 copy.416
  102.0 24.7 %gather_fusion = f32[4096]{0:T(1024)S(1)} fusion(f32[128]{0:T(128)S(1)} %get-tuple-element.269, s32[4096]{0:T(1024)S(1)} %get-tuple-element.280), kind=kCustom, calls=%fused_computation | custom fusion | bytes 49152 | tf_op jit(solution)/shard_map/gather | solution.py:373
  126.8 0.6 broadcast_select_fusion.12
  127.4 4.4 %all-to-all-start.1 = ((f32[128,32,1]{1,2,0:T(1,128)}), f32[128,32,1]{1,2,0:T(1,128)S(1)}, u32[]{:S(2)}, u32[]{:S(2)}) async-start(f32[128,32,1]{1,2,0:T(1,128)} %bitcast.36), calls=%async_computation.1 | async-start | bytes 131072 | tf_op jit(solution)/shard_map/all_to_all | solution.py:376
  131.8 16.2 %gather_fusion.3 = f32[4096,256]{1,0:T(8,128)} fusion(f32[768,256]{1,0:T(8,128)S(1)} %copy.416, s32[4096]{0:T(1024)S(1)} %get-tuple-element.279), kind=kCustom, calls=%fused_computation.3 | custom fusion | bytes 8404992 | tf_op jit(solution)/shard_map/gather | solution.py:372
  148.1 3.9 %broadcast_multiply_fusion = f32[128,32,256]{2,1,0:T(8,128)} fusion(f32[128,32,256]{2,1,0:T(8,128)} %bitcast.548, f32[128,32]{1,0:T(8,128)S(1)} %convert_bitcast_fusion), kind=kLoop, calls=%fused_computation.12 | loop fusion | flops 1048576 | bytes 8404992 | tf_op jit(solution)/shard_map/mul | solution.py:372
  152.0 10.2 %all-to-all-start.2 = ((f32[128,32,256]{2,1,0:T(8,128)}), f32[128,32,256]{2,1,0:T(8,128)}, u32[]{:S(2)}, u32[]{:S(2)}) async-start(f32[128,32,256]{2,1,0:T(8,128)} %broadcast_multiply_fusion), calls=%async_computation.2 | async-start | bytes 8388608 | tf_op jit(solution)/shard_map/all_to_all | solution.py:375
  162.9 6.5 %gather_fusion.2 = f32[768]{0:T(1024)} fusion(f32[128]{0:T(128)S(1)} %get-tuple-element.269, s32[1024]{0:T(1024)S(1)} %pad_clamp_fusion.6), kind=kCustom, calls=%fused_computation.2 | custom fusion | bytes 9216 | tf_op jit(solution)/shard_map/gather | solution.py:354
  169.6 1.0 gather_fusion.5
  170.6 1.5 gather_fusion.6
  172.1 1.7 gather_fusion.7
  173.8 1.7 gather_fusion.8
  175.4 1.6 gather_fusion.9
  177.1 1.6 gather_fusion.10
  178.7 0.5 fusion.14
  179.3 1.0 fusion.4
  180.4 0.6 fusion.69
  181.3 0.6 broadcast.2022
  181.9 1.7 reduce.51
  183.6 4.5 %gather_fusion.1 = f32[768]{0:T(1024)S(1)} fusion(f32[4096]{0:T(1024)S(1)} %all_to_all.21, s32[1024]{0:T(1024)S(1)} %pad_clamp_fusion.7), kind=kCustom, calls=%fused_computation.1 | custom fusion | bytes 9216 | tf_op jit(solution)/shard_map/gather | solution.py:382
  188.2 26.7 %all-to-all-done.2 = f32[128,32,256]{2,1,0:T(8,128)} async-done(((f32[128,32,256]{2,1,0:T(8,128)}), f32[128,32,256]{2,1,0:T(8,128)}, u32[]{:S(2)}, u32[]{:S(2)}) %all-to-all-start.2) | async-done | bytes 4194336 | tf_op jit(solution)/shard_map/all_to_all | solution.py:375
  214.8 4.3 %gather_fusion.4 = f32[768,256]{1,0:T(8,128)S(1)} fusion(f32[4096,256]{1,0:T(8,128)} %bitcast.50, s32[1024]{0:T(1024)S(1)} %pad_clamp_fusion.7), kind=kCustom, calls=%fused_computation.4 | custom fusion | bytes 1575936 | tf_op jit(solution)/shard_map/gather | solution.py:380
  219.1 0.2 broadcast_select_fusion
  219.6 0.2 copy-done.32
  221.1 1.8 fusion.25
  223.1 1.2 constant_dynamic-slice_fusion
  224.4 1.8 fusion.27
  226.4 0.2 scatter-add.54
  226.7 0.2 scatter-add.55
  226.8 1.9 broadcast_select_fusion.4
  228.7 1.3 scatter-add.56
  230.0 0.1 divide_add_fusion
  230.2 0.2 scatter-add.59
  230.3 1.4 copy.446
  (180 shorter events, 4.4 us)
Async XLA Ops:
  6.1 95.6 %all-to-all-start = ((s32[128,32,1]{1,2,0:T(1,128)}), s32[128,32,1]{1,2,0:T(1,128)S(1)}, u32[]{:S(2)}, u32[]{:S(2)}) async-start(s32[128,32,1]{1,2,0:T(1,128)} %bitcast.32), calls=%async_computation | async-start | bytes 131072 | tf_op jit(solution)/shard_map/all_to_all | solution.py:369
  18.5 1.6 copy-start.24
  86.4 6.9 %copy-start.20 = (f32[128]{0:T(128)S(1)}, f32[128]{0:T(128)}, u32[]{:S(2)}) copy-start(f32[128]{0:T(128)} %param.38) | copy-start | bytes 1540
  86.4 6.9 %copy-start.33 = (f32[128]{0:T(128)S(1)}, f32[128]{0:T(128)}, u32[]{:S(2)}) copy-start(f32[128]{0:T(128)} %param.37) | copy-start | bytes 1540
  86.4 7.4 %copy-start.17 = (f32[8,8,1,1]{1,0,3,2:T(8,128)S(1)}, f32[8,8,1,1]{1,0,3,2:T(8,128)}, u32[]{:S(2)}) copy-start(f32[8,8,1,1]{1,0,3,2:T(8,128)} %constant.556) | copy-start | bytes 772
  86.4 11.2 %copy-start.36 = (s32[5]{0:T(128)S(1)}, s32[5]{0:T(128)}, u32[]{:S(2)}) copy-start(s32[5]{0:T(128)} %constant.550.clone.1) | copy-start | bytes 64
  88.0 12.1 %copy-start.34 = (s32[5]{0:T(128)S(1)}, s32[5]{0:T(128)}, u32[]{:S(2)}) copy-start(s32[5]{0:T(128)} %constant.552.clone.1) | copy-start | bytes 64
  88.0 12.1 %copy-start.35 = (s32[5]{0:T(128)S(1)}, s32[5]{0:T(128)}, u32[]{:S(2)}) copy-start(s32[5]{0:T(128)} %constant.554.clone.1) | copy-start | bytes 64
  127.4 24.6 %all-to-all-start.1 = ((f32[128,32,1]{1,2,0:T(1,128)}), f32[128,32,1]{1,2,0:T(1,128)S(1)}, u32[]{:S(2)}, u32[]{:S(2)}) async-start(f32[128,32,1]{1,2,0:T(1,128)} %bitcast.36), calls=%async_computation.1 | async-start | bytes 131072 | tf_op jit(solution)/shard_map/all_to_all | solution.py:376
  152.0 10.3 %copy-start.13 = (f32[128,4,1,8,8]{0,4,3,2,1:T(8,128)S(1)}, f32[128,4,1,8,8]{0,4,3,2,1:T(8,128)}, u32[]{:S(2)}) copy-start(f32[128,4,1,8,8]{0,4,3,2,1:T(8,128)} %get-tuple-element.189) | copy-start | bytes 393220
  152.0 10.4 %copy-start.12 = (f32[128,4,1,8,8]{0,4,3,2,1:T(8,128)S(1)}, f32[128,4,1,8,8]{0,4,3,2,1:T(8,128)}, u32[]{:S(2)}) copy-start(f32[128,4,1,8,8]{0,4,3,2,1:T(8,128)} %get-tuple-element.188) | copy-start | bytes 393220
  152.0 10.5 %copy-start.15 = (f32[128,4,8,1,8]{0,4,3,2,1:T(8,128)S(1)}, f32[128,4,8,1,8]{0,4,3,2,1:T(8,128)}, u32[]{:S(2)}) copy-start(f32[128,4,8,1,8]{0,4,3,2,1:T(8,128)} %get-tuple-element.184) | copy-start | bytes 393220
  152.0 10.6 %copy-start.14 = (f32[128,4,8,1,8]{0,4,3,2,1:T(8,128)S(1)}, f32[128,4,8,1,8]{0,4,3,2,1:T(8,128)}, u32[]{:S(2)}) copy-start(f32[128,4,8,1,8]{0,4,3,2,1:T(8,128)} %get-tuple-element.185) | copy-start | bytes 393220
  152.0 10.6 %copy-start.16 = (f32[128,32,1]{1,2,0:T(1,128)}, f32[128,32,1]{1,2,0:T(1,128)S(1)}, u32[]{:S(2)}) copy-start(f32[128,32,1]{1,2,0:T(1,128)S(1)} %all-to-all-done.1) | copy-start | bytes 49156
  152.0 62.8 %all-to-all-start.2 = ((f32[128,32,256]{2,1,0:T(8,128)}), f32[128,32,256]{2,1,0:T(8,128)}, u32[]{:S(2)}, u32[]{:S(2)}) async-start(f32[128,32,256]{2,1,0:T(8,128)} %broadcast_multiply_fusion), calls=%async_computation.2 | async-start | bytes 8388608 | tf_op jit(solution)/shard_map/all_to_all | solution.py:375
  162.3 7.2 %copy-start = (f32[128,1,8,8,8]{0,3,4,2,1:T(8,128)S(1)}, f32[128,1,8,8,8]{0,3,4,2,1:T(8,128)}, u32[]{:S(2)}) copy-start(f32[128,1,8,8,8]{0,3,4,2,1:T(8,128)} %fusion.1) | copy-start | bytes 786436
  169.5 9.8 %copy-start.1 = (f32[128,8,8,8]{0,3,2,1:T(8,128)S(1)}, f32[128,8,8,8]{0,3,2,1:T(8,128)}, u32[]{:S(2)}) copy-start(f32[128,8,8,8]{0,3,2,1:T(8,128)} %fusion.13) | copy-start | bytes 786436
  169.6 10.7 %copy-start.2 = (f32[128,1,8,8,8]{0,4,3,2,1:T(8,128)S(1)}, f32[128,1,8,8,8]{0,4,3,2,1:T(8,128)}, u32[]{:S(2)}) copy-start(f32[128,1,8,8,8]{0,4,3,2,1:T(8,128)} %fusion) | copy-start | bytes 786436
  172.1 8.3 %copy-start.26 = (s32[6,128]{1,0:T(8,128)S(1)}, s32[6,128]{1,0:T(8,128)}, u32[]{:S(2)}) copy-start(s32[6,128]{1,0:T(8,128)} %param.35) | copy-start | bytes 9220
  172.1 8.9 %copy-start.18 = (s32[6,128]{1,0:T(8,128)S(1)}, s32[6,128]{1,0:T(8,128)}, u32[]{:S(2)}) copy-start(s32[6,128]{1,0:T(8,128)} %param.36) | copy-start | bytes 9220
  173.8 7.3 %copy-start.3 = (f32[128,256]{1,0:T(8,128)S(1)}, f32[128,256]{1,0:T(8,128)}, u32[]{:S(2)}) copy-start(f32[128,256]{1,0:T(8,128)} %gather_fusion.6) | copy-start | bytes 393220
  175.4 5.7 %copy-start.4 = (f32[128,256]{1,0:T(8,128)S(1)}, f32[128,256]{1,0:T(8,128)}, u32[]{:S(2)}) copy-start(f32[128,256]{1,0:T(8,128)} %gather_fusion.7) | copy-start | bytes 393220
  177.1 4.1 %copy-start.5 = (f32[128,256]{1,0:T(8,128)S(1)}, f32[128,256]{1,0:T(8,128)}, u32[]{:S(2)}) copy-start(f32[128,256]{1,0:T(8,128)} %gather_fusion.8) | copy-start | bytes 393220
  178.7 2.5 %copy-start.6 = (f32[128,256]{1,0:T(8,128)S(1)}, f32[128,256]{1,0:T(8,128)}, u32[]{:S(2)}) copy-start(f32[128,256]{1,0:T(8,128)} %gather_fusion.9) | copy-start | bytes 393220
  178.7 2.5 %copy-start.7 = (f32[128,256]{1,0:T(8,128)S(1)}, f32[128,256]{1,0:T(8,128)}, u32[]{:S(2)}) copy-start(f32[128,256]{1,0:T(8,128)} %gather_fusion.10) | copy-start | bytes 393220
  180.3 7.8 %copy-start.19 = (s32[6,128]{1,0:T(8,128)S(1)}, s32[6,128]{1,0:T(8,128)}, u32[]{:S(2)}) copy-start(s32[6,128]{1,0:T(8,128)} %param.36) | copy-start | bytes 9220
  180.4 7.7 %copy-start.23 = (f32[768]{0:T(1024)S(1)}, f32[768]{0:T(1024)}, u32[]{:S(2)}) copy-start(f32[768]{0:T(1024)} %gather_fusion.2) | copy-start | bytes 9220
  219.1 0.7 copy-start.32
  219.1 0.9 copy-start.31
  219.3 1.4 copy-start.30
  219.4 1.5 copy-start.29
  219.6 1.4 copy-start.28
  219.8 1.2 copy-start.11
  219.8 1.2 copy-start.22
  219.8 1.2 copy-start.25
  219.8 1.2 copy-start.21
  219.8 1.3 copy-start.10
  220.0 3.0 %copy-start.9 = (f32[128,4,8,8]{0,3,2,1:T(8,128)S(1)}, f32[128,4,8,8]{0,3,2,1:T(8,128)}, u32[]{:S(2)}) copy-start(f32[128,4,8,8]{0,3,2,1:T(8,128)} %get-tuple-element.183) | copy-start | bytes 393220
  220.0 4.2 %copy-start.27 = (pred[128]{0:T(512)(128)(4,1)S(1)}, pred[128]{0:T(512)(128)(4,1)}, u32[]{:S(2)}) copy-start(pred[128]{0:T(512)(128)(4,1)} %get-tuple-element.240) | copy-start | bytes 388
  220.1 4.2 %copy-start.8 = (f32[128,4,8,8]{0,3,2,1:T(8,128)S(1)}, f32[128,4,8,8]{0,3,2,1:T(8,128)}, u32[]{:S(2)}) copy-start(f32[128,4,8,8]{0,3,2,1:T(8,128)} %get-tuple-element.182) | copy-start | bytes 393220

commit v2 on v1

v2 whole, which is shorter than its diff:
```python
import functools

import jax
import jax.numpy as jnp
import numpy as np
from jax import lax
from jax.experimental import pallas as pl
from jax.experimental.pallas import tpu as pltpu
from jax.sharding import PartitionSpec as P

NP = 8
HCAP = 32
MESH = pl.DeviceIdType.MESH
HIGHEST = lax.Precision.HIGHEST

metric_scale = 0.25


def gll_tables(poly_order):
    num_points = poly_order + 1
    points = -np.cos(np.pi * np.arange(num_points) / poly_order)
    legendre = np.zeros((num_points, num_points))
    for sweeps in range(101):
        legendre[:, 0] = 1.0
        legendre[:, 1] = points
        for degree in range(2, num_points):
            legendre[:, degree] = (
                (2 * degree - 1) * points * legendre[:, degree - 1]
                - (degree - 1) * legendre[:, degree - 2]
            ) / degree
        if sweeps < 100:
            points = points - (points * legendre[:, poly_order] - legendre[:, poly_order - 1]) / (
                num_points * legendre[:, poly_order]
            )
    end_values = legendre[:, poly_order]
    weights = 2.0 / (poly_order * num_points * end_values**2)
    distance = points[:, None] - points[None, :] + np.eye(num_points)
    derivative = end_values[:, None] / end_values[None, :] / distance
    derivative = derivative * (1.0 - np.eye(num_points))
    derivative[0, 0] = -poly_order * num_points / 4.0
    derivative[poly_order, poly_order] = poly_order * num_points / 4.0
    return (points, weights, derivative)


def fixed_tables():
    derivative = gll_tables(NP - 1)[2]
    take = np.zeros((2, 4, 128, 128))
    for end in range(2):
        for first in range(8):
            for second in range(8):
                face_lane = 64 * end + 8 * first + second
                half, chunk = 64 * (first % 2), first // 2
                take[0, chunk, half + 56 * end + second, face_lane] = 1.0
                take[1, chunk, half + 8 * second + 7 * end, face_lane] = 1.0
    turns = np.zeros((3, 128, 128))
    for end in range(2):
        for first in range(8):
            for second in range(8):
                to = 64 * end + 8 * first + second
                turns[0, 64 * end + 8 * (7 - first) + second, to] = 1.0
                turns[1, 64 * end + 8 * first + 7 - second, to] = 1.0
                turns[2, 64 * end + 8 * second + first, to] = 1.0
    eye2, eye8 = np.eye(2), np.eye(8)
    inside = [
        np.kron(eye2, np.kron(derivative.T, eye8)),
        np.kron(eye2, np.kron(eye8, derivative.T)),
    ]
    lift = np.swapaxes(take, 2, 3)
    stack = [take.reshape(8, 128, 128), lift.reshape(8, 128, 128), turns, np.stack(inside)]
    return np.concatenate(stack).astype(np.float32)


TAKE, LIFT, TURN, INSIDE, TABLES = 0, 8, 16, 19, 21
NEAR, FAR, GIVE, CODE, WALL, Z_IN, BULK, THIN, KEPT = 0, 6, 12, 18, 21, 24, 25, 26, 27

def my_place():
    group = lax.axis_index("grp")
    member = lax.axis_index("dev")
    return group, member // 8, (member // 2) % 4, member % 2


def chip_at(place, step):
    z_at, y_at, x_at, _ = place
    x_to = (x_at + step) % 4
    y_to = (y_at + step // 4 + step) % 4
    z_to = (z_at + step // 16 + step // 4 + step) % 4
    return z_to, y_to * 4 + x_to


def permute_kernel(place_ref, state_ref, send_ref, sem):
    def one(slot, carry):
        at = place_ref[slot]
        pltpu.make_async_copy(
            state_ref.at[slot], send_ref.at[pl.ds((at % 8) * 16, 16), at // 8], sem
        ).start()
        return carry

    lax.fori_loop(0, 256, one, 0, unroll=8)
    pltpu.make_async_copy(state_ref, state_ref, sem).wait()


def exact(left, right):
    return jnp.dot(left, right, precision=HIGHEST, preferred_element_type=jnp.float32)


def prepare(mine, near_ref, turn_ref, wall_ref, bulk_ref, dens_ref, stack, kept, lane, sub):
    near_rows = near_ref[...]
    wall_rows = wall_ref[...]
    away_rows = jnp.where((near_rows // 128 != mine) & (wall_rows == 0), 1.0, 0.0)
    stack[...] = jnp.zeros((128, 128), jnp.float32)
    stack[0:6, :] = near_rows.astype(jnp.float32)
    stack[8:14, :] = turn_ref[...].astype(jnp.float32)
    stack[16:22, :] = wall_rows.astype(jnp.float32)
    stack[24:25, :] = bulk_ref[...]
    stack[25:26, :] = dens_ref[...]
    stack[26:32, :] = away_rows
    columns = stack[...].T
    away_all = stack[...]
    upper = (sub < lane).astype(jnp.float32)
    give_rank = jnp.dot(away_all, upper, preferred_element_type=jnp.float32)
    base = (mine * 128).astype(jnp.float32)
    lane_f = lane.astype(jnp.float32)
    sub_f = sub.astype(jnp.float32)
    for face in range(6):
        near = columns[:, face : face + 1]
        away = columns[:, 26 + face : 27 + face]
        away_row = away_rows[face : face + 1, :]
        kept[NEAR + face] = jnp.where((near - base == lane_f) & (away == 0.0), 1.0, 0.0)
        before = jnp.where((near_rows[face : face + 1, :].astype(jnp.float32) < near), away_row, 0.0)
        take_rank = jnp.sum(before, axis=1, keepdims=True)
        kept[FAR + face] = jnp.where((take_rank == lane_f) & (away > 0.0), 1.0, 0.0)
        row_rank = give_rank[26 + face : 27 + face, :]
        kept[GIVE + face] = jnp.where((row_rank == sub_f) & (away_row > 0.0), 1.0, 0.0)
    low = lane < 64
    for axis in range(3):
        kept[CODE + axis] = jnp.where(
            low, columns[:, 8 + 2 * axis : 9 + 2 * axis], columns[:, 9 + 2 * axis : 10 + 2 * axis]
        )
        kept[WALL + axis] = jnp.where(
            low, columns[:, 16 + 2 * axis : 17 + 2 * axis], columns[:, 17 + 2 * axis : 18 + 2 * axis]
        )
    bulk = jnp.broadcast_to(columns[:, 24:25], (128, 128))
    dens = jnp.broadcast_to(columns[:, 25:26], (128, 128))
    kept[Z_IN] = jnp.sqrt(bulk * dens)
    kept[BULK] = bulk
    kept[THIN] = 1.0 / dens


def exchange_kernel(
    note_ref,
    send_ref,
    near_ref,
    turn_ref,
    wall_ref,
    bulk_ref,
    dens_ref,
    fixed_ref,
    out_ref,
    notes,
    first,
    second,
    third,
    table,
    index,
    perm,
    fixed,
    stack,
    facing,
    kept,
    field,
    traces,
    ask,
    ask_in,
    answer,
    answer_in,
    total,
    sems,
):
    load_fixed = pltpu.make_async_copy(fixed_ref, fixed, sems.at[14])
    load_fixed.start()
    place = my_place()
    mine = place[0] * 32 + lax.axis_index("dev")
    core = place[3]
    barrier = pltpu.get_barrier_semaphore()

    def other(step):
        group, chip = chip_at(place, step // 2)
        member = chip * 2 + (core + step) % 2
        return group, member

    def greet(step, carry):
        group, member = other(step)
        pl.semaphore_signal(barrier, inc=1, device_id=(group, member), device_id_type=MESH)
        return carry

    lax.fori_loop(1, 128, greet, 0)
    pl.semaphore_wait(barrier, 127)

    def copy(source, target, phase, group, member):
        pltpu.make_async_remote_copy(
            src_ref=source,
            dst_ref=target,
            send_sem=sems.at[2 * phase],
            recv_sem=sems.at[2 * phase + 1],
            device_id=(group, member),
            device_id_type=MESH,
        ).start()

    def finish(buffer, rows, which):
        view = buffer.at[pl.ds(0, rows)]
        pltpu.make_async_copy(view, view, sems.at[which]).wait()

    def tell(step, carry):
        group, member = other(step)
        copy(note_ref.at[pl.ds(group * 32 + member, 1)], notes.at[pl.ds(mine, 1)], 0, group, member)
        return carry

    lax.fori_loop(1, 128, tell, 0)

    def spread(group, member):
        copy(send_ref.at[group * 32 + member], first.at[pl.ds(mine * 32, 32)], 1, group, member)

    spread(place[0], lax.axis_index("dev") + 1 - 2 * core)
    for side in range(2):

        def spread_step(step, carry):
            group, chip = chip_at(place, step)
            spread(group, chip * 2 + side)
            return carry

        lax.fori_loop(1, 64, spread_step, 0)
    notes[pl.ds(mine, 1)] = note_ref[pl.ds(mine, 1)]
    first[pl.ds(mine * 32, 32)] = send_ref[mine]

    finish(notes, 127, 1)
    note = notes.reshape(128, 128)[...]
    lane = lax.broadcasted_iota(jnp.int32, (128, 128), 1)
    sub = lax.broadcasted_iota(jnp.int32, (128, 128), 0)
    lower = (lane < sub).astype(jnp.float32)
    piece = jnp.zeros((128, 128), jnp.int32)
    for k in range(32):
        piece = piece + jnp.where(note[:, 32 + k : 33 + k] == lane, k + 1, 0)
    valid = piece > 0
    rank = jnp.dot(lower, valid.astype(jnp.float32), preferred_element_type=jnp.float32)
    rank = rank.astype(jnp.int32)
    entry = sub * 32 + piece - 1
    for j in range(16):
        table[j : j + 1, :] = jnp.sum(
            jnp.where(valid & (rank == j), entry, 0), axis=0, keepdims=True
        )
    to_scalar = pltpu.make_async_copy(table, index, sems.at[8])
    to_scalar.start()
    has = jnp.broadcast_to(note[:, 0:1] > 0, (128, 128))
    order = jnp.dot(lower, has.astype(jnp.float32), preferred_element_type=jnp.float32)
    slot = jnp.where(has & (order.astype(jnp.int32) == lane), 1.0, 0.0)[:, :16]
    rows = []
    for i in range(8):
        is_row = (note[:, i : i + 1] - 1 == lane).astype(jnp.float32)
        rows.append(
            lax.dot_general(
                slot, is_row, (((0,), (0,)), ((), ())), preferred_element_type=jnp.float32
            )
        )
    perm[...] = jnp.concatenate(rows, axis=0).T
    facing[...] = note.astype(jnp.float32).T
    prepare(mine, near_ref, turn_ref, wall_ref, bulk_ref, dens_ref, stack, kept, lane, sub)
    ask[...] = jnp.zeros((256, 1, 128), jnp.float32)
    load_fixed.wait()
    to_scalar.wait()

    finish(first, 127 * 32, 3)

    def pick(target, base, at):
        for j in range(16):
            target[pl.ds(base + j, 1)] = first[pl.ds(index[j, at], 1)]

    pick(third, mine * 16, mine)

    def forward(step):
        group, member = other(step)
        at = group * 32 + member
        copy(
            second.at[pl.ds(at * 16, 16)], third.at[pl.ds(mine * 16, 16)], 2, group, member
        )

    def pick_step(step, carry):
        group, member = other(step)
        at = group * 32 + member
        pick(second, at * 16, at)

        @pl.when(step > 1)
        def _():
            forward(step - 1)

        return carry

    lax.fori_loop(1, 128, pick_step, 0)
    forward(127)
    finish(third, 127 * 16, 5)

    arrived = third.reshape(8, 16, 16, 128)
    for part in range(16):
        field[part] = exact(perm[...], arrived[:, part].reshape(128, 128))

    low = lane < 64
    sign = jnp.where(low, -1.0, 1.0)
    z_in = kept[Z_IN]

    def pair(axis, which):
        if axis == 0:
            return jnp.where(low, field[which], field[12 + which])
        found = exact(field[which], fixed[TAKE + 4 * (axis - 1)])
        for q in range(1, 4):
            found = found + exact(field[4 * q + which], fixed[TAKE + 4 * (axis - 1) + q])
        return found

    for axis in range(3):
        pressure = pair(axis, 0)
        normal = sign * pair(axis, 1 + axis)
        traces[6 + 2 * axis] = pressure
        traces[7 + 2 * axis] = normal
        turned = pltpu.roll(pressure + z_in * normal, 64, 1)
        traces[2 * axis] = jnp.where(low, z_in, turned)
        traces[2 * axis + 1] = jnp.where(low, turned, z_in)

    ask_rows = ask.reshape(256, 128)
    for face in range(6):
        if face < 4:
            ask_rows[pl.ds(64 * face, 32, stride=2), :] = exact(
                kept[GIVE + face][:32], traces[face]
            )
        else:
            ask_rows[pl.ds(128 * (face - 4) + 1, 16, stride=8), :] = exact(
                kept[GIVE + face][:16], traces[face]
            )

    def swap(source, target, phase):
        def one(step, carry):
            group, member = other(step)
            copy(
                source.at[pl.ds((group * 32 + member) * 2, 2)],
                target.at[pl.ds(mine * 2, 2)],
                phase,
                group,
                member,
            )
            return carry

        lax.fori_loop(1, 128, one, 0)
        target[pl.ds(mine * 2, 2)] = source[pl.ds(mine * 2, 2)]

    swap(ask, ask_in, 4 + 1)

    scale = jnp.float32(-metric_scale) * kept[BULK]
    thin = jnp.float32(-metric_scale) * kept[THIN]
    derivative = gll_tables(NP - 1)[2]

    def along_x(which):
        straight = [field[4 * q + which] for q in range(4)]
        crossed = [pltpu.roll(part, 64, 1) for part in straight]
        sums = []
        for q in range(4):
            found = None
            for b in range(4):
                one = jnp.where(low, derivative[2 * q, 2 * b], derivative[2 * q + 1, 2 * b + 1])
                two = jnp.where(low, derivative[2 * q, 2 * b + 1], derivative[2 * q + 1, 2 * b])
                term = one.astype(jnp.float32) * straight[b] + two.astype(jnp.float32) * crossed[b]
                found = term if found is None else found + term
            sums.append(found)
        return sums

    side_x = along_x(1)
    grad_x = along_x(0)
    for q in range(4):
        side = side_x[q] + exact(field[4 * q + 2], fixed[INSIDE])
        side = side + exact(field[4 * q + 3], fixed[INSIDE + 1])
        total[4 * q] = scale * side
        total[4 * q + 1] = thin * grad_x[q]
        total[4 * q + 2] = thin * exact(field[4 * q], fixed[INSIDE])
        total[4 * q + 3] = thin * exact(field[4 * q], fixed[INSIDE + 1])

    finish(ask_in, 254, 11)
    asked = ask_in.reshape(256, 128)
    answer_rows = answer.reshape(256, 128)
    sub_f = sub.astype(jnp.float32)
    for spot in range(2):
        face = mine // 32 if spot == 0 else 4 + mine // 64
        to = facing[pl.ds(8 + face, 1), :] - 1.0
        chosen = (to == sub_f).astype(jnp.float32)
        answer_rows[pl.ds(spot, 128, stride=2), :] = exact(
            chosen, asked[pl.ds(spot, 128, stride=2), :]
        )
    swap(answer, answer_in, 4 + 2)

    outside = [exact(kept[NEAR + face], traces[face ^ 1]) for face in range(6)]

    finish(answer_in, 254, 13)
    answers = answer_in.reshape(256, 128)
    for face in range(6):
        if face < 4:
            brought = answers[pl.ds(64 * (face ^ 1), 32, stride=2), :]
            picked = exact(kept[FAR + face][:, :32], brought)
        else:
            brought = answers[pl.ds(128 * ((face ^ 1) - 4) + 1, 16, stride=8), :]
            picked = exact(kept[FAR + face][:, :16], brought)
        outside[face] = outside[face] + picked
    lift = jnp.float32(metric_scale / float(gll_tables(NP - 1)[1][0]))
    gain_p = []
    gain_u = []
    for axis in range(3):
        even, odd = outside[2 * axis], outside[2 * axis + 1]
        coming = jnp.where(low, even, odd)
        z_out = pltpu.roll(jnp.where(low, odd, even), 64, 1)
        code = kept[CODE + axis].astype(jnp.int32)
        coming = jnp.where(code % 2 == 1, exact(coming, fixed[TURN]), coming)
        coming = jnp.where(code // 2 % 2 == 1, exact(coming, fixed[TURN + 1]), coming)
        coming = jnp.where(code >= 4, exact(coming, fixed[TURN + 2]), coming)
        is_wall = kept[WALL + axis] == 1.0
        pressure = traces[6 + 2 * axis]
        normal = traces[7 + 2 * axis]
        z_out = jnp.where(is_wall, z_in, z_out)
        jump = jnp.where(is_wall, 2.0 * z_in * normal, coming - pressure + z_out * normal)
        jump = lift * jump / (z_in + z_out)
        gain_p.append(kept[BULK] * jump)
        gain_u.append(-sign * kept[THIN] * z_in * jump)
    for q in range(4):
        for which in range(4):
            part = total[4 * q + which]
            for axis in range(3):
                if which == 0:
                    gain = gain_p[axis]
                elif which == 1 + axis:
                    gain = gain_u[axis]
                else:
                    continue
                if axis > 0:
                    part = part + exact(gain, fixed[LIFT + 4 * (axis - 1) + q])
                elif q == 0:
                    part = part + jnp.where(low, gain, 0.0)
                elif q == 3:
                    part = part + jnp.where(low, 0.0, gain)
            out_ref[pl.ds(4 * q + which, 128, stride=16), :] = part
    finish(notes, 127, 0)
    finish(first, 127 * 32, 2)
    finish(third, 127 * 16, 4)
    finish(ask_in, 254, 10)
    finish(answer_in, 254, 12)


def body(old_state, dest_row, neighbours, orientation, wall_flags, bulk_modulus, density):
    mine = lax.axis_index("grp") * 32 + lax.axis_index("dev")
    below = dest_row[None, :] < dest_row[:, None]
    tie = (dest_row[None, :] == dest_row[:, None]) & (
        jnp.arange(256)[None, :] < jnp.arange(256)[:, None]
    )
    position = jnp.sum((below | tie).astype(jnp.int32), axis=1)
    ordered = jnp.sum(
        jnp.where(position[:, None] == jnp.arange(256)[None, :], dest_row[:, None], 0), axis=0
    )
    pieces = ordered.reshape(32, 8)
    targets = pieces[:, 0] // 128
    row_ids = jnp.sum(
        jnp.where(
            targets[None, :, None] == jnp.arange(128)[:, None, None], pieces[None] % 128 + 1, 0
        ),
        axis=1,
    )
    owners = neighbours // 128
    beside = jnp.max(jnp.where((owners != mine) & (wall_flags == 0), owners + 1, 0), axis=1)
    note = jnp.concatenate(
        [
            row_ids,
            jnp.broadcast_to(beside[None, :], (128, 6)),
            jnp.zeros((128, 18), jnp.int32),
            jnp.broadcast_to(targets[None, :], (128, 32)),
            jnp.zeros((128, 64), jnp.int32),
        ],
        axis=1,
    )[:, None, :]
    view = old_state.reshape(256, 4, 4, 128).transpose(0, 2, 1, 3).reshape(256, 16, 1, 128)
    whole = pl.BlockSpec(memory_space=pltpu.VMEM)
    sends = pl.pallas_call(
        permute_kernel,
        out_shape=jax.ShapeDtypeStruct((128, 32, 1, 128), jnp.float32),
        in_specs=[pl.BlockSpec(memory_space=pltpu.SMEM), pl.BlockSpec(memory_space=pl.ANY)],
        out_specs=whole,
        scratch_shapes=[pltpu.SemaphoreType.DMA],
    )(position, view)
    small = pltpu.VMEM((256, 1, 128), jnp.float32)
    result = pl.pallas_call(
        exchange_kernel,
        out_shape=jax.ShapeDtypeStruct((2048, 128), jnp.float32),
        in_specs=[whole] * 7 + [pl.BlockSpec(memory_space=pl.ANY)],
        out_specs=whole,
        scratch_shapes=[
            pltpu.VMEM((128, 1, 128), jnp.int32),
            pltpu.VMEM((4096, 1, 128), jnp.float32),
            pltpu.VMEM((2048, 1, 128), jnp.float32),
            pltpu.VMEM((2048, 1, 128), jnp.float32),
            pltpu.VMEM((16, 128), jnp.int32),
            pltpu.SMEM((16, 128), jnp.int32),
            pltpu.VMEM((128, 128), jnp.float32),
            pltpu.VMEM((TABLES, 128, 128), jnp.float32),
            pltpu.VMEM((128, 128), jnp.float32),
            pltpu.VMEM((128, 128), jnp.float32),
            pltpu.VMEM((KEPT, 128, 128), jnp.float32),
            pltpu.VMEM((16, 128, 128), jnp.float32),
            pltpu.VMEM((12, 128, 128), jnp.float32),
            small,
            small,
            small,
            small,
            pltpu.VMEM((16, 128, 128), jnp.float32),
            pltpu.SemaphoreType.DMA((15,)),
        ],
        compiler_params=pltpu.CompilerParams(collective_id=0, has_side_effects=True),
    )(
        note,
        sends,
        neighbours,
        orientation,
        wall_flags,
        bulk_modulus[None, :],
        density[None, :],
        jnp.asarray(fixed_tables()),
    )
    return result.reshape(128, 4, 4, 128).transpose(0, 2, 1, 3).reshape(128, 4, 512)


def solution(mesh):
    in_specs = (
        P(("grp", "dev"), None, None),
        P(("grp", "dev")),
        P(None, ("grp", "dev")),
        P(None, ("grp", "dev")),
        P(None, ("grp", "dev")),
        P(("grp", "dev")),
        P(("grp", "dev")),
    )
    out_specs = P(("grp", "dev"), None, None)
    return jax.shard_map(body, mesh=mesh, in_specs=in_specs, out_specs=out_specs, check_vma=False)
```

time: 233 us -> 95.8 us (0.41)
  local copies, waits for them, and re-layouts: 85 us -> 3.43 us
  waiting for transfers between devices: 26.7 us -> 0 us
  starting transfers between devices: 26.1 us -> 0 us
  Pallas kernels: 65.5 us -> 89.3 us
  other arithmetic: 21.8 us -> 2.74 us
  matrix products: 5.26 us -> 0 us
    gather x12 -> x0, local copies, waits for them, and re-layouts: 65.4 us -> none  [the longest x2 24.8 us: body(): answer_imped = impedance[serve_at % elem_dev] * asked]
    all_to_all x3 -> x0, waiting for transfers between devices: 26.7 us -> none  [the longest x1 26.7 us: body(): lax.all_to_all(answer, ('grp', 'dev'), split_axis=0, concat_axis=0, tiled...]
    all_to_all x3 -> x0, starting transfers between devices: 26.1 us -> none  [the longest x1 11.5 us: body(): lax.all_to_all(requests_out, ('grp', 'dev'), split_axis=0, concat_axis=0,...]
    pallas_call x2, Pallas kernels: 65.5 us -> 89.3 us  [the longest x1 84.4 us: body(): pl.pallas_call(exchange_kernel, out_shape=jax.ShapeDtypeStruct((2048, 128...]
    another operation x14 -> x0, local copies, waits for them, and re-layouts: 6.93 us -> none
    dot_general x6 -> x0, matrix products: 5.26 us -> none  [derivative_along(): jnp.einsum(einsum_forms[axis_id], matrix, scalar_field, precision=lax.Pre...]
    mul x5 -> x0, other arithmetic: 5.11 us -> none  [the longest x1 3.9 us: body(): answer = trace_table[serve_at] * asked[:, None]]
    scatter-add x8 -> x0, other arithmetic: 3.85 us -> none  [the longest x4 3.72 us: right_side(): result.at[(slice(None), 0) + face_index(face_id)]]
  transfers between devices with their start and end apart: 3 -> 0, of which waited for: 1 -> 0; matrix products, arithmetic and copies ran while one was open for 28% -> 0% of each run, Pallas kernels for 28% -> 0%
where the time goes in v2:
time: 95.8 us; the launch traced here: 95.5 us
  Pallas kernels  89.3 us (93%)
  local copies, waits for them, and re-layouts  3.43 us (4%)
  other arithmetic  2.74 us (3%)
    pallas_call x1, Pallas kernels, body(): pl.pallas_call(exchange_kernel, out_shape=jax.ShapeDtypeStruct((2048, 128...  84.4 us
    pallas_call x1, Pallas kernels, body(): pl.pallas_call(permute_kernel, out_shape=jax.ShapeDtypeStruct((128, 32, 1...  4.9 us
    unnamed x3, local copies, waits for them, and re-layouts  2.27 us

profile of v2, /device:TPU:1, one launch (start us, length us, event | category | flops | bytes accessed | tf_op | source)
XLA Modules:
  0.0 95.5 jit_solution(3938983905794600341)
XLA Ops:
  0.0 0.8 select_reduce_fusion.2
  0.8 0.9 convert_reduce_fusion.place_ref
  1.8 0.0 copy-start
  1.8 0.8 select_reduce_fusion
  2.6 0.1 reshape.128
  2.7 0.1 slice_reduce_fusion
  2.9 0.1 copy.16
  3.0 0.1 select_reduce_fusion.1
  3.1 0.1 copy.17
  3.2 0.8 concatenate.3
  4.0 0.0 copy-done
  4.0 4.9 %shard_map.82.send_ref = f32[128,32,1,128]{3,2,1,0:T(1,128)} custom-call(s32[256]{0:T(256)} %copy-done, f32[256,16,1,128]{3,2,1,0:T(1,128)} %bitcast.14), custom_call_target="tpu_custom_call" | custom-call | tf_op jit(solution)/shard_map/pallas_call | solution.py:482
  8.9 84.4 %shard_map.83 = f32[2048,128]{1,0:T(8,128)} custom-call(s32[128,1,128]{2,1,0:T(1,128)} %bitcast.15, f32[128,32,1,128]{3,2,1,0:T(1,128)} %shard_map.82.send_ref, s32[6,128]{1,0:T(8,128)} %near_ref.1, s32[6,128]{1,0:T(8,128)} %turn_ref.1, s32[6,128]{1,0:T(8,128)} %wall_ref.1, f32[1,128]{1,0:T(1,128)} %bitcast.16, f32[1,128]{1,0:T(1,128)} %bitcast.17, ...), custom_call_target="tpu_custom_call" | custom-call | tf_op jit(solution)/shard_map/pallas_call | solution.py:490
  93.3 2.3 %copy.21 = f32[128,4,512]{2,1,0:T(4,128)} copy(f32[128,4,512]{2,1,0:T(4,128)} %bitcast.13) | data formatting | bytes 2097152
  (7 shorter events, 0.1 us)
Async XLA Ops:
  1.8 2.2 %copy-start = (s32[256]{0:T(256)}, s32[256]{0:T(256)S(1)}, u32[]{:S(2)}) copy-start(s32[256]{0:T(256)S(1)} %convert_reduce_fusion.place_ref) | copy-start | bytes 3076

commit v3 on v2

v3 whole, which is shorter than its diff:
```python
import jax
import jax.numpy as jnp
import numpy as np
from jax import lax
from jax.experimental import pallas as pl
from jax.experimental.pallas import tpu as pltpu
from jax.sharding import PartitionSpec as P

NP = 8
MESH = pl.DeviceIdType.MESH
HIGHEST = lax.Precision.HIGHEST

metric_scale = 0.25


def gll_tables(poly_order):
    num_points = poly_order + 1
    points = -np.cos(np.pi * np.arange(num_points) / poly_order)
    legendre = np.zeros((num_points, num_points))
    for sweeps in range(101):
        legendre[:, 0] = 1.0
        legendre[:, 1] = points
        for degree in range(2, num_points):
            legendre[:, degree] = (
                (2 * degree - 1) * points * legendre[:, degree - 1]
                - (degree - 1) * legendre[:, degree - 2]
            ) / degree
        if sweeps < 100:
            points = points - (points * legendre[:, poly_order] - legendre[:, poly_order - 1]) / (
                num_points * legendre[:, poly_order]
            )
    end_values = legendre[:, poly_order]
    weights = 2.0 / (poly_order * num_points * end_values**2)
    distance = points[:, None] - points[None, :] + np.eye(num_points)
    derivative = end_values[:, None] / end_values[None, :] / distance
    derivative = derivative * (1.0 - np.eye(num_points))
    derivative[0, 0] = -poly_order * num_points / 4.0
    derivative[poly_order, poly_order] = poly_order * num_points / 4.0
    return (points, weights, derivative)


def fixed_tables():
    derivative = gll_tables(NP - 1)[2]
    take = np.zeros((2, 4, 128, 128))
    for end in range(2):
        for first in range(8):
            for second in range(8):
                face_lane = 64 * end + 8 * first + second
                half, chunk = 64 * (first % 2), first // 2
                take[0, chunk, half + 56 * end + second, face_lane] = 1.0
                take[1, chunk, half + 8 * second + 7 * end, face_lane] = 1.0
    turns = np.zeros((3, 128, 128))
    for end in range(2):
        for first in range(8):
            for second in range(8):
                to = 64 * end + 8 * first + second
                turns[0, 64 * end + 8 * (7 - first) + second, to] = 1.0
                turns[1, 64 * end + 8 * first + 7 - second, to] = 1.0
                turns[2, 64 * end + 8 * second + first, to] = 1.0
    eye2, eye8 = np.eye(2), np.eye(8)
    inside = [
        np.kron(eye2, np.kron(derivative.T, eye8)),
        np.kron(eye2, np.kron(eye8, derivative.T)),
    ]
    lift = np.swapaxes(take, 2, 3)
    stack = [take.reshape(8, 128, 128), lift.reshape(8, 128, 128), turns]
    return np.concatenate(stack), np.stack(inside).astype(np.float32)


TAKE, LIFT, TURN = 0, 8, 16
NEAR, FAR, GIVE = 0, 6, 12
CODE, WALL, Z_IN, BULK, THIN, KEPT = 0, 3, 6, 7, 8, 9

STEPS = sorted(
    [(a, b, c, d) for a in range(4) for b in range(4) for c in range(4) for d in range(2)][1:],
    key=lambda step: -sum(min(part, 4 - part) for part in step[:3]),
)


def my_place():
    group = lax.axis_index("grp")
    member = lax.axis_index("dev")
    return group, member // 8, (member // 2) % 4, member % 2


def chip_at(place, step):
    z_at, y_at, x_at, _ = place
    x_to = (x_at + step) % 4
    y_to = (y_at + step // 4 + step) % 4
    z_to = (z_at + step // 16 + step // 4 + step) % 4
    return z_to, y_to * 4 + x_to


def split3(value):
    high = value.astype(jnp.bfloat16)
    rest = value - high.astype(jnp.float32)
    middle = rest.astype(jnp.bfloat16)
    low = (rest - middle.astype(jnp.float32)).astype(jnp.bfloat16)
    return high, middle, low


def pick_rows(chosen, value):
    wide = value.shape[1]
    parts = jnp.concatenate(split3(value), axis=1)
    found = jnp.dot(chosen, parts, preferred_element_type=jnp.float32)
    return found[:, :wide] + found[:, wide : 2 * wide] + found[:, 2 * wide :]


def pick_lanes(value, chosen):
    tall = value.shape[0]
    parts = jnp.concatenate(split3(value), axis=0)
    found = jnp.dot(parts, chosen, preferred_element_type=jnp.float32)
    return found[:tall] + found[tall : 2 * tall] + found[2 * tall :]


def exact(left, right):
    return jnp.dot(left, right, precision=HIGHEST, preferred_element_type=jnp.float32)


def count(left, right):
    return jnp.dot(
        left.astype(jnp.bfloat16), right.astype(jnp.bfloat16), preferred_element_type=jnp.float32
    )


def order_slots(dest_row, stack, ranks):
    lane = lax.broadcasted_iota(jnp.int32, (128, 128), 1)
    sub = lax.broadcasted_iota(jnp.int32, (128, 128), 0)
    value = dest_row.astype(jnp.float32)
    stack[0:2, :] = value
    columns = stack[...].T
    rows = [value[0:1, :], value[1:2, :]]
    slots = []
    for half in range(2):
        mine = columns[:, half : half + 1]
        below = jnp.zeros((128, 128), jnp.float32)
        for other in range(2):
            tied = rows[other] == mine
            if other > half:
                less = rows[other] < mine
            elif other < half:
                less = (rows[other] < mine) | tied
            else:
                less = (rows[other] < mine) | (tied & (lane < sub))
            below = below + jnp.where(less, 1.0, 0.0)
        slots.append((mine, jnp.sum(below, axis=1, keepdims=True)))
    lane_f = lane.astype(jnp.float32)
    sub_f = sub.astype(jnp.float32)
    for half in range(2):
        found = jnp.zeros((1, 128), jnp.float32)
        for part in range(2):
            is_it = slots[part][1] == lane_f + 128.0 * half
            found = found + jnp.sum(
                jnp.where(is_it, sub_f + 128.0 * part, 0.0), axis=0, keepdims=True
            )
        ranks[half : half + 1, :] = jnp.clip(found.astype(jnp.int32), 0, 255)
    return rows, slots


def write_notes(rows, slots, near_rows, wall_rows, mine, note_out):
    lane = lax.broadcasted_iota(jnp.int32, (128, 128), 1)
    sub = lax.broadcasted_iota(jnp.int32, (128, 128), 0)
    lane_f = lane.astype(jnp.float32)
    sub_f = sub.astype(jnp.float32)
    note = jnp.zeros((128, 128), jnp.float32)
    heads = jnp.zeros((1, 128), jnp.float32)
    for half in range(2):
        row = rows[half].astype(jnp.int32)
        owner_row = jnp.where(row >= 0, row // 128, -1)
        to = jnp.where(owner_row == sub, 1.0, 0.0)
        mine_f, rank = slots[half]
        column = mine_f.astype(jnp.int32)
        rank_i = rank.astype(jnp.int32)
        owner = jnp.where(column >= 0, column // 128, -1).astype(jnp.float32)
        inside = (column % 128 + 1).astype(jnp.float32)
        ids = jnp.where((rank_i % 8) == lane, inside, 0.0)
        note = note + count(to, ids)
        heads = heads + jnp.sum(
            jnp.where(rank_i == 8 * (lane - 32), owner, 0.0), axis=0, keepdims=True
        )
    owners = near_rows // 128
    beside = jnp.where((owners != mine) & (wall_rows == 0), owners + 1, 0).astype(jnp.float32)
    beside = jnp.max(beside, axis=1, keepdims=True)
    beside = jnp.sum(
        jnp.where(lane_f[:6] == sub_f[:6] + 8.0, beside, 0.0), axis=0, keepdims=True
    )
    heads = jnp.where((lane[:1] >= 32) & (lane[:1] < 64), heads, 0.0)
    note_out.reshape(128, 128)[...] = (note + heads + beside).astype(jnp.int32)


def prepare(mine, near_rows, turn_rows, wall_rows, bulk_row, dens_row, stack, moves, kept):
    lane = lax.broadcasted_iota(jnp.int32, (128, 128), 1)
    sub = lax.broadcasted_iota(jnp.int32, (128, 128), 0)
    away_rows = jnp.where((near_rows // 128 != mine) & (wall_rows == 0), 1.0, 0.0)
    stack[0:6, :] = near_rows.astype(jnp.float32)
    stack[8:14, :] = turn_rows.astype(jnp.float32)
    stack[16:22, :] = wall_rows.astype(jnp.float32)
    stack[24:25, :] = bulk_row
    stack[25:26, :] = dens_row
    stack[26:32, :] = away_rows
    columns = stack[...].T
    give_rank = count(stack[24:32, :], (sub < lane).astype(jnp.float32))
    base = (mine * 128).astype(jnp.float32)
    lane_f = lane.astype(jnp.float32)
    sub_f = sub.astype(jnp.float32)
    for face in range(6):
        near = columns[:, face : face + 1]
        away = columns[:, 26 + face : 27 + face]
        away_row = away_rows[face : face + 1, :]
        is_near = (near - base == lane_f) & (away == 0.0)
        before = jnp.where((near_rows[face : face + 1, :].astype(jnp.float32) < near), away_row, 0.0)
        take_rank = jnp.sum(before, axis=1, keepdims=True)
        is_far = (take_rank == lane_f) & (away > 0.0)
        is_given = (give_rank[2 + face : 3 + face, :] == sub_f) & (away_row > 0.0)
        moves[NEAR + face] = jnp.where(is_near, 1.0, 0.0).astype(jnp.bfloat16)
        moves[FAR + face] = jnp.where(is_far, 1.0, 0.0).astype(jnp.bfloat16)
        moves[GIVE + face] = jnp.where(is_given, 1.0, 0.0).astype(jnp.bfloat16)
    low = lane < 64
    for axis in range(3):
        kept[CODE + axis] = jnp.where(
            low, columns[:, 8 + 2 * axis : 9 + 2 * axis], columns[:, 9 + 2 * axis : 10 + 2 * axis]
        )
        kept[WALL + axis] = jnp.where(
            low, columns[:, 16 + 2 * axis : 17 + 2 * axis], columns[:, 17 + 2 * axis : 18 + 2 * axis]
        )
    bulk = jnp.broadcast_to(columns[:, 24:25], (128, 128))
    dens = jnp.broadcast_to(columns[:, 25:26], (128, 128))
    kept[Z_IN] = jnp.sqrt(bulk * dens)
    kept[BULK] = bulk
    kept[THIN] = 1.0 / dens


def exchange_kernel(
    state_ref, dest_ref, near_ref, turn_ref, wall_ref, bulk_ref, dens_ref, fixed_ref, inside_ref,
    out_ref, state, dest, near, turn, wall, bulk, dens, fixed, inside, ranks, slot_of, note_out,
    notes, sends, first, second, third, table, index, perm, stack, facing, moves, kept, field,
    traces, ask, ask_in, answer, answer_in, total, sems, loads, met_y, met_z,
):
    place = my_place()
    z_at, y_at, x_at, core = place
    member_here = lax.axis_index("dev")
    mine = z_at * 32 + member_here
    barrier = pltpu.get_barrier_semaphore()

    def signal(sem, group, y_to, x_to, core_to):
        pl.semaphore_signal(
            sem, inc=1, device_id=(group, (y_to * 4 + x_to) * 2 + core_to), device_id_type=MESH
        )

    for step in range(1, 8):
        signal(barrier, z_at, y_at, (x_at + step // 2) % 4, (core + step) % 2)
    for step in range(1, 4):
        signal(barrier, z_at, (y_at + step) % 4, x_at, core)
        signal(barrier, (z_at + step) % 4, y_at, x_at, core)

    pairs = [
        (dest_ref, dest), (near_ref, near), (wall_ref, wall), (turn_ref, turn),
        (bulk_ref, bulk), (dens_ref, dens), (state_ref, state), (fixed_ref, fixed),
        (inside_ref, inside),
    ]
    local = [pltpu.make_async_copy(a, b, loads.at[n]) for n, (a, b) in enumerate(pairs)]
    for one in local:
        one.start()
    stack[...] = jnp.zeros((128, 128), jnp.float32)
    local[0].wait()
    rows, slots = order_slots(dest[...], stack, ranks)
    to_slots = pltpu.make_async_copy(ranks, slot_of, loads.at[9])
    to_slots.start()
    pl.semaphore_wait(barrier, 13)
    for step in range(1, 4):
        signal(met_y, z_at, (y_at + step) % 4, x_at, core)
    local[1].wait()
    local[2].wait()
    write_notes(rows, slots, near[...], wall[...], mine, note_out)
    pl.semaphore_wait(met_y, 3)
    for step in range(1, 4):
        signal(met_z, (z_at + step) % 4, y_at, x_at, core)
    to_slots.wait()
    local[6].wait()

    def gather_first(target, base, at):
        row, chunk = at // 16, at % 16
        found = []
        for k in range(32):
            slot = slot_of[k // 16, (k % 16) * 8 + row]
            found.append(state[pl.ds(slot * 16 + chunk, 1)])
        for k in range(32):
            target[pl.ds(base + k, 1)] = found[k]

    def to_device(step):
        chip_step = jnp.where(step > 63, step - 63, step)
        side = jnp.where(step == 0, 1 - core, step // 64)
        group, chip = chip_at(place, chip_step)
        return group, chip * 2 + side

    def copy(source, target, phase, group, member):
        pltpu.make_async_remote_copy(
            src_ref=source,
            dst_ref=target,
            send_sem=sems.at[2 * phase],
            recv_sem=sems.at[2 * phase + 1],
            device_id=(group, member),
            device_id_type=MESH,
        ).start()

    def finish(buffer, rows, which):
        view = buffer.at[pl.ds(0, rows)]
        pltpu.make_async_copy(view, view, sems.at[which]).wait()

    def fetch(step):
        group, member = to_device(step)
        at = group * 32 + member
        gather_first(sends, at * 32, at)

    def spread(step):
        group, member = to_device(step)
        at = group * 32 + member
        copy(sends.at[pl.ds(at * 32, 32)], first.at[pl.ds(mine * 32, 32)], 1, group, member)

    def tell(group, member):
        at = group * 32 + member
        copy(note_out.at[pl.ds(at, 1)], notes.at[pl.ds(mine, 1)], 0, group, member)

    fetch(0)
    fetch(1)
    pl.semaphore_wait(met_z, 3)
    spread(0)
    tell(z_at, member_here + 1 - 2 * core)

    def early(step, carry):
        fetch(step + 1)
        spread(step)
        group, chip = chip_at(place, step)
        tell(group, chip * 2)
        tell(group, chip * 2 + 1)
        return carry

    lax.fori_loop(1, 64, early, 0)

    def late(step, carry):
        fetch(step + 1)
        spread(step)
        return carry

    lax.fori_loop(64, 126, late, 0)
    spread(126)
    gather_first(first, mine * 32, mine)
    notes[pl.ds(mine, 1)] = note_out[pl.ds(mine, 1)]

    local[3].wait()
    local[4].wait()
    local[5].wait()
    prepare(
        mine, near[...], turn[...], wall[...], bulk[...], dens[...], stack, moves, kept
    )
    ask[...] = jnp.zeros((256, 1, 128), jnp.float32)
    finish(notes, 127, 1)
    note = notes.reshape(128, 128)[...]
    lane = lax.broadcasted_iota(jnp.int32, (128, 128), 1)
    sub = lax.broadcasted_iota(jnp.int32, (128, 128), 0)
    lower = (lane < sub).astype(jnp.float32)
    piece = jnp.zeros((128, 128), jnp.int32)
    for k in range(32):
        piece = piece + jnp.where(note[:, 32 + k : 33 + k] == lane, k + 1, 0)
    valid = piece > 0
    rank = count(lower, valid.astype(jnp.float32)).astype(jnp.int32)
    entry = sub * 32 + piece - 1
    for j in range(16):
        chosen = jnp.sum(jnp.where(valid & (rank == j), entry, 0), axis=0, keepdims=True)
        table[j : j + 1, :] = jnp.clip(chosen, 0, 4095)
    to_index = pltpu.make_async_copy(table, index, loads.at[10])
    to_index.start()
    has = jnp.broadcast_to(note[:, 0:1] > 0, (128, 128))
    order = count(lower, has.astype(jnp.float32)).astype(jnp.int32)
    slot = jnp.where(has & (order == lane), 1.0, 0.0)[:, :16]
    rows = []
    for i in range(8):
        is_row = (note[:, i : i + 1] - 1 == lane).astype(jnp.float32)
        rows.append(
            lax.dot_general(
                slot, is_row, (((0,), (0,)), ((), ())), preferred_element_type=jnp.float32
            )
        )
    perm[...] = jnp.concatenate(rows, axis=0).T.astype(jnp.bfloat16)
    facing[...] = note.astype(jnp.float32).T
    local[7].wait()
    local[8].wait()
    to_index.wait()
    finish(first, 127 * 32, 3)

    def gather_second(target, base, at):
        found = [first[pl.ds(index[j, at], 1)] for j in range(16)]
        for j in range(16):
            target[pl.ds(base + j, 1)] = found[j]

    def device_at(step):
        group = (z_at + step[0]) % 4
        chip = ((y_at + step[1]) % 4) * 4 + (x_at + step[2]) % 4
        return group, chip * 2 + (core + step[3]) % 2

    def forward(group, member):
        at = group * 32 + member
        copy(
            second.at[pl.ds(at * 16, 16)], third.at[pl.ds(mine * 16, 16)], 2, group, member
        )

    before = None
    for step in STEPS:
        group, member = device_at(step)
        at = group * 32 + member
        gather_second(second, at * 16, at)
        if before is not None:
            forward(*before)
        before = (group, member)
    gather_second(third, mine * 16, mine)
    forward(*before)
    finish(third, 127 * 16, 5)

    arrived = third.reshape(8, 16, 16, 128)
    for part in range(16):
        field[part] = pick_rows(perm[...], arrived[:, part].reshape(128, 128))

    low = lane < 64
    sign = jnp.where(low, -1.0, 1.0)
    z_in = kept[Z_IN]

    def pair(axis, which):
        if axis == 0:
            return jnp.where(low, field[which], field[12 + which])
        found = pick_lanes(field[which], fixed[TAKE + 4 * (axis - 1)])
        for q in range(1, 4):
            found = found + pick_lanes(field[4 * q + which], fixed[TAKE + 4 * (axis - 1) + q])
        return found

    ask_rows = ask.reshape(256, 128)
    for axis in range(3):
        pressure = pair(axis, 0)
        normal = sign * pair(axis, 1 + axis)
        traces[6 + 2 * axis] = pressure
        traces[7 + 2 * axis] = normal
        turned = pltpu.roll(pressure + z_in * normal, 64, 1)
        traces[2 * axis] = jnp.where(low, z_in, turned)
        traces[2 * axis + 1] = jnp.where(low, turned, z_in)
        for face in (2 * axis, 2 * axis + 1):
            if face < 4:
                ask_rows[pl.ds(64 * face, 32, stride=2), :] = pick_rows(
                    moves[GIVE + face][:32], traces[face]
                )
            else:
                ask_rows[pl.ds(128 * (face - 4) + 1, 16, stride=8), :] = pick_rows(
                    moves[GIVE + face][:16], traces[face]
                )

    def swap(source, target, phase):
        for step in STEPS:
            group, member = device_at(step)
            copy(
                source.at[pl.ds((group * 32 + member) * 2, 2)],
                target.at[pl.ds(mine * 2, 2)],
                phase,
                group,
                member,
            )
        target[pl.ds(mine * 2, 2)] = source[pl.ds(mine * 2, 2)]

    swap(ask, ask_in, 3)

    scale = jnp.float32(-metric_scale) * kept[BULK]
    thin = jnp.float32(-metric_scale) * kept[THIN]
    derivative = gll_tables(NP - 1)[2]

    def along_x(which):
        straight = [field[4 * q + which] for q in range(4)]
        crossed = [pltpu.roll(part, 64, 1) for part in straight]
        sums = []
        for q in range(4):
            found = None
            for b in range(4):
                one = jnp.where(low, derivative[2 * q, 2 * b], derivative[2 * q + 1, 2 * b + 1])
                two = jnp.where(low, derivative[2 * q, 2 * b + 1], derivative[2 * q + 1, 2 * b])
                term = one.astype(jnp.float32) * straight[b] + two.astype(jnp.float32) * crossed[b]
                found = term if found is None else found + term
            sums.append(found)
        return sums

    side_x = along_x(1)
    grad_x = along_x(0)
    for q in range(4):
        side = side_x[q] + exact(field[4 * q + 2], inside[0])
        side = side + exact(field[4 * q + 3], inside[1])
        total[4 * q] = scale * side
        total[4 * q + 1] = thin * grad_x[q]
        total[4 * q + 2] = thin * exact(field[4 * q], inside[0])
        total[4 * q + 3] = thin * exact(field[4 * q], inside[1])

    finish(ask_in, 254, 7)
    asked = ask_in.reshape(256, 128)
    answer_rows = answer.reshape(256, 128)
    sub_f = sub.astype(jnp.float32)
    for spot in range(2):
        face = mine // 32 if spot == 0 else 4 + mine // 64
        to = facing[pl.ds(8 + face, 1), :] - 1.0
        chosen = jnp.where(to == sub_f, 1.0, 0.0).astype(jnp.bfloat16)
        answer_rows[pl.ds(spot, 128, stride=2), :] = pick_rows(
            chosen, asked[pl.ds(spot, 128, stride=2), :]
        )
    swap(answer, answer_in, 4)

    outside = [pick_rows(moves[NEAR + face], traces[face ^ 1]) for face in range(6)]

    finish(answer_in, 254, 9)
    answers = answer_in.reshape(256, 128)
    for face in range(6):
        if face < 4:
            brought = answers[pl.ds(64 * (face ^ 1), 32, stride=2), :]
            picked = pick_rows(moves[FAR + face][:, :32], brought)
        else:
            brought = answers[pl.ds(128 * ((face ^ 1) - 4) + 1, 16, stride=8), :]
            picked = pick_rows(moves[FAR + face][:, :16], brought)
        outside[face] = outside[face] + picked
    lift = jnp.float32(metric_scale / float(gll_tables(NP - 1)[1][0]))
    gains = []
    for axis in range(3):
        even, odd = outside[2 * axis], outside[2 * axis + 1]
        coming = jnp.where(low, even, odd)
        z_out = pltpu.roll(jnp.where(low, odd, even), 64, 1)
        code = kept[CODE + axis].astype(jnp.int32)
        coming = jnp.where(code % 2 == 1, pick_lanes(coming, fixed[TURN]), coming)
        coming = jnp.where(code // 2 % 2 == 1, pick_lanes(coming, fixed[TURN + 1]), coming)
        coming = jnp.where(code >= 4, pick_lanes(coming, fixed[TURN + 2]), coming)
        is_wall = kept[WALL + axis] == 1.0
        pressure = traces[6 + 2 * axis]
        normal = traces[7 + 2 * axis]
        z_out = jnp.where(is_wall, z_in, z_out)
        jump = jnp.where(is_wall, 2.0 * z_in * normal, coming - pressure + z_out * normal)
        jump = lift * jump / (z_in + z_out)
        gains.append(jnp.concatenate([kept[BULK] * jump, -sign * kept[THIN] * z_in * jump]))
    for q in range(4):
        if q == 0:
            along = jnp.where(jnp.concatenate([low, low]), gains[0], 0.0)
        elif q == 3:
            along = jnp.where(jnp.concatenate([low, low]), 0.0, gains[0])
        else:
            along = None
        lifted = [along] + [
            pick_lanes(gains[axis], fixed[LIFT + 4 * (axis - 1) + q]) for axis in (1, 2)
        ]
        part = total[4 * q] + lifted[1][:128] + lifted[2][:128]
        part_x = total[4 * q + 1]
        if along is not None:
            part = part + along[:128]
            part_x = part_x + along[128:]
        out_ref[pl.ds(4 * q, 128, stride=16), :] = part
        out_ref[pl.ds(4 * q + 1, 128, stride=16), :] = part_x
        out_ref[pl.ds(4 * q + 2, 128, stride=16), :] = total[4 * q + 2] + lifted[1][128:]
        out_ref[pl.ds(4 * q + 3, 128, stride=16), :] = total[4 * q + 3] + lifted[2][128:]
    finish(notes, 127, 0)
    finish(first, 127 * 32, 2)
    finish(third, 127 * 16, 4)
    finish(ask_in, 254, 6)
    finish(answer_in, 254, 8)


def body(old_state, dest_row, neighbours, orientation, wall_flags, bulk_modulus, density):
    view = old_state.reshape(256, 4, 4, 128).transpose(0, 2, 1, 3).reshape(4096, 1, 128)
    picks, inside = fixed_tables()
    f32, i32, bf16 = jnp.float32, jnp.int32, jnp.bfloat16
    halo = pltpu.VMEM((256, 1, 128), f32)
    result = pl.pallas_call(
        exchange_kernel,
        out_shape=jax.ShapeDtypeStruct((2048, 128), f32),
        in_specs=[pl.BlockSpec(memory_space=pl.ANY)] * 9,
        out_specs=pl.BlockSpec(memory_space=pltpu.VMEM),
        scratch_shapes=[
            pltpu.VMEM((4096, 1, 128), f32),
            pltpu.VMEM((2, 128), i32),
            pltpu.VMEM((6, 128), i32),
            pltpu.VMEM((6, 128), i32),
            pltpu.VMEM((6, 128), i32),
            pltpu.VMEM((1, 128), f32),
            pltpu.VMEM((1, 128), f32),
            pltpu.VMEM((19, 128, 128), bf16),
            pltpu.VMEM((2, 128, 128), f32),
            pltpu.VMEM((2, 128), i32),
            pltpu.SMEM((2, 128), i32),
            pltpu.VMEM((128, 1, 128), i32),
            pltpu.VMEM((128, 1, 128), i32),
            pltpu.VMEM((4096, 1, 128), f32),
            pltpu.VMEM((4096, 1, 128), f32),
            pltpu.VMEM((2048, 1, 128), f32),
            pltpu.VMEM((2048, 1, 128), f32),
            pltpu.VMEM((16, 128), i32),
            pltpu.SMEM((16, 128), i32),
            pltpu.VMEM((128, 128), bf16),
            pltpu.VMEM((128, 128), f32),
            pltpu.VMEM((128, 128), f32),
            pltpu.VMEM((18, 128, 128), bf16),
            pltpu.VMEM((KEPT, 128, 128), f32),
            pltpu.VMEM((16, 128, 128), f32),
            pltpu.VMEM((12, 128, 128), f32),
            halo,
            halo,
            halo,
            halo,
            pltpu.VMEM((16, 128, 128), f32),
            pltpu.SemaphoreType.DMA((10,)),
            pltpu.SemaphoreType.DMA((11,)),
            pltpu.SemaphoreType.REGULAR,
            pltpu.SemaphoreType.REGULAR,
        ],
        compiler_params=pltpu.CompilerParams(collective_id=0, has_side_effects=True),
    )(
        view,
        dest_row.reshape(2, 128),
        neighbours,
        orientation,
        wall_flags,
        bulk_modulus[None, :],
        density[None, :],
        jnp.asarray(picks, bf16),
        jnp.asarray(inside),
    )
    return result.reshape(128, 4, 4, 128).transpose(0, 2, 1, 3).reshape(128, 4, 512)


def solution(mesh):
    in_specs = (
        P(("grp", "dev"), None, None),
        P(("grp", "dev")),
        P(None, ("grp", "dev")),
        P(None, ("grp", "dev")),
        P(None, ("grp", "dev")),
        P(("grp", "dev")),
        P(("grp", "dev")),
    )
    out_specs = P(("grp", "dev"), None, None)
    return jax.shard_map(body, mesh=mesh, in_specs=in_specs, out_specs=out_specs, check_vma=False)
```

time: 95.8 us -> 73.3 us (0.77)
  Pallas kernels: 89.3 us -> 70.9 us
  other arithmetic: 2.74 us -> 0 us
  local copies, waits for them, and re-layouts: 3.43 us -> 2.26 us
    pallas_call x1, Pallas kernels: 84.4 us -> 70.9 us  [body(): pl.pallas_call(exchange_kernel, out_shape=jax.ShapeDtypeStruct((2048, 128...]
    pallas_call x1 -> x0, Pallas kernels: 4.9 us -> none  [body(): pl.pallas_call(permute_kernel, out_shape=jax.ShapeDtypeStruct((128, 32, 1...]
    reduce_sum x3 -> x0, other arithmetic: 1.87 us -> none  [the longest x1 0.93 us: body(): position = jnp.sum((below | tie).astype(jnp.int32), axis=1)]
    unnamed x3 -> x1, local copies, waits for them, and re-layouts: 2.27 us -> 2.26 us
where the time goes in v3:
time: 73.3 us; the launch traced here: 73.2 us
  Pallas kernels  70.9 us (97%)
  local copies, waits for them, and re-layouts  2.26 us (3%)
    pallas_call x1, Pallas kernels, body(): pl.pallas_call(exchange_kernel, out_shape=jax.ShapeDtypeStruct((2048, 128...  70.9 us
    unnamed x1, local copies, waits for them, and re-layouts  2.26 us

profile of v3, /device:TPU:1, one launch (start us, length us, event | category | flops | bytes accessed | tf_op | source)
XLA Modules:
  0.0 73.2 jit_solution(7400391008625758563)
XLA Ops:
  0.0 70.9 %shard_map.91 = f32[2048,128]{1,0:T(8,128)} custom-call(f32[4096,1,128]{2,1,0:T(1,128)} %bitcast.14, s32[2,128]{1,0:T(2,128)} %bitcast.15, s32[6,128]{1,0:T(8,128)} %near_ref.1, s32[6,128]{1,0:T(8,128)} %turn_ref.1, s32[6,128]{1,0:T(8,128)} %wall_ref.1, f32[1,128]{1,0:T(1,128)} %bitcast.16, f32[1,128]{1,0:T(1,128)} %bitcast.17, ...), custom_call_target="tpu_custom_call" | custom-call | tf_op jit(solution)/shard_map/pallas_call | solution.py:569
  70.9 2.3 %copy.13 = f32[128,4,512]{2,1,0:T(4,128)} copy(f32[128,4,512]{2,1,0:T(4,128)} %bitcast.13) | data formatting | bytes 2097152

commit v4 on v3

--- a/solution.py
+++ b/solution.py
@@ -9,6 +9,7 @@
 NP = 8
 MESH = pl.DeviceIdType.MESH
 HIGHEST = lax.Precision.HIGHEST
+HELD = 48
 
 metric_scale = 0.25
 
@@ -64,17 +65,24 @@
     ]
     lift = np.swapaxes(take, 2, 3)
     stack = [take.reshape(8, 128, 128), lift.reshape(8, 128, 128), turns]
-    return np.concatenate(stack), np.stack(inside).astype(np.float32)
+    comes_from = np.full((128, 128), -1.0)
+    for number, step in enumerate(NEARBY):
+        for device in range(128):
+            place = device // 32, device // 8 % 4, device // 2 % 4, device % 2
+            back = [(at - by) % size for at, by, size in zip(place, step, (4, 4, 4, 2))]
+            comes_from[number, device] = back[0] * 32 + back[1] * 8 + back[2] * 2 + back[3]
+    return np.concatenate(stack), np.stack(inside + [comes_from]).astype(np.float32)
 
 
 TAKE, LIFT, TURN = 0, 8, 16
-NEAR, FAR, GIVE = 0, 6, 12
-CODE, WALL, Z_IN, BULK, THIN, KEPT = 0, 3, 6, 7, 8, 9
+NEAR, FAR, GIVE, ROUTE, OWNER = 0, 3, 6, 9, 12
+CODE, WALL, Z_IN, BULK, THIN, SPOT, KEPT = 0, 3, 6, 7, 8, 9, 12
 
 STEPS = sorted(
     [(a, b, c, d) for a in range(4) for b in range(4) for c in range(4) for d in range(2)][1:],
     key=lambda step: -sum(min(part, 4 - part) for part in step[:3]),
 )
+NEARBY = [(0, 0, 0, 0)] + STEPS[::-1][:31]
 
 
 def my_place():
@@ -188,7 +196,9 @@
     note_out.reshape(128, 128)[...] = (note + heads + beside).astype(jnp.int32)
 
 
-def prepare(mine, near_rows, turn_rows, wall_rows, bulk_row, dens_row, stack, moves, kept):
+def prepare(
+    mine, near_rows, turn_rows, wall_rows, bulk_row, dens_row, comes_from, stack, moves, kept
+):
     lane = lax.broadcasted_iota(jnp.int32, (128, 128), 1)
     sub = lax.broadcasted_iota(jnp.int32, (128, 128), 0)
     away_rows = jnp.where((near_rows // 128 != mine) & (wall_rows == 0), 1.0, 0.0)
@@ -203,18 +213,31 @@
     base = (mine * 128).astype(jnp.float32)
     lane_f = lane.astype(jnp.float32)
     sub_f = sub.astype(jnp.float32)
+    owners = near_rows // 128
+    beside = jnp.where(away_rows > 0.0, owners + 1, 0).astype(jnp.float32)
+    beside = jnp.max(beside, axis=1, keepdims=True) - 1.0
     for face in range(6):
+        axis, half = face // 2, face % 2
         near = columns[:, face : face + 1]
         away = columns[:, 26 + face : 27 + face]
         away_row = away_rows[face : face + 1, :]
         is_near = (near - base == lane_f) & (away == 0.0)
         before = jnp.where((near_rows[face : face + 1, :].astype(jnp.float32) < near), away_row, 0.0)
         take_rank = jnp.sum(before, axis=1, keepdims=True)
-        is_far = (take_rank == lane_f) & (away > 0.0)
-        is_given = (give_rank[2 + face : 3 + face, :] == sub_f) & (away_row > 0.0)
-        moves[NEAR + face] = jnp.where(is_near, 1.0, 0.0).astype(jnp.bfloat16)
-        moves[FAR + face] = jnp.where(is_far, 1.0, 0.0).astype(jnp.bfloat16)
-        moves[GIVE + face] = jnp.where(is_given, 1.0, 0.0).astype(jnp.bfloat16)
+        is_far = jnp.where((take_rank == lane_f) & (away > 0.0), 1.0, 0.0)
+        passed_by = jnp.where(comes_from == beside[face : face + 1, :], 1.0, 0.0)
+        is_given = (give_rank[2 + face : 3 + face, :] == sub_f[:32]) & (away_row > 0.0)
+        rows = pl.ds(128 * half, 128)
+        moves[NEAR + axis, rows] = jnp.where(is_near, 1.0, 0.0).astype(jnp.bfloat16)
+        moves[FAR + axis, rows] = count(is_far[:, :32], passed_by).astype(jnp.bfloat16)
+        moves[GIVE + axis, pl.ds(32 * (1 - half), 32)] = jnp.where(is_given, 1.0, 0.0).astype(
+            jnp.bfloat16
+        )
+        near_i = near.astype(jnp.int32)
+        moves[OWNER + axis, rows] = jnp.where(near_i // 128 == lane, 1.0, 0.0).astype(jnp.bfloat16)
+        kept[SPOT + axis, :, 64 * half : 64 * half + 64] = jnp.broadcast_to(
+            (near_i % 128).astype(jnp.float32), (128, 64)
+        )
     low = lane < 64
     for axis in range(3):
         kept[CODE + axis] = jnp.where(
@@ -233,7 +256,7 @@
 def exchange_kernel(
     state_ref, dest_ref, near_ref, turn_ref, wall_ref, bulk_ref, dens_ref, fixed_ref, inside_ref,
     out_ref, state, dest, near, turn, wall, bulk, dens, fixed, inside, ranks, slot_of, note_out,
-    notes, sends, first, second, third, table, index, perm, stack, facing, moves, kept, field,
+    notes, sends, first, second, third, table, index, perm, stack, z_here, z_all, moves, kept, field,
     traces, ask, ask_in, answer, answer_in, total, sems, loads, met_y, met_z,
 ):
     place = my_place()
@@ -312,10 +335,17 @@
         at = group * 32 + member
         gather_first(sends, at * 32, at)
 
-    def spread(step):
+    def spread(step, leaves):
         group, member = to_device(step)
         at = group * 32 + member
-        copy(sends.at[pl.ds(at * 32, 32)], first.at[pl.ds(mine * 32, 32)], 1, group, member)
+        pltpu.make_async_remote_copy(
+            src_ref=sends.at[pl.ds(at * 32, 32)],
+            dst_ref=first.at[pl.ds(mine * 32, 32)],
+            send_sem=sems.at[leaves],
+            recv_sem=sems.at[16 + member % 2],
+            device_id=(group, member),
+            device_id_type=MESH,
+        ).start()
 
     def tell(group, member):
         at = group * 32 + member
@@ -324,36 +354,52 @@
     fetch(0)
     fetch(1)
     pl.semaphore_wait(met_z, 3)
-    spread(0)
+    spread(0, 2)
     tell(z_at, member_here + 1 - 2 * core)
 
-    def early(step, carry):
+    def early(leaves):
+        def one(step, carry):
+            fetch(step + 1)
+            spread(step, leaves)
+            group, chip = chip_at(place, step)
+            tell(group, chip * 2)
+            tell(group, chip * 2 + 1)
+            return carry
+
+        return one
+
+    lax.fori_loop(1, HELD + 1, early(12), 0)
+    lax.fori_loop(HELD + 1, 64, early(13), 0)
+
+    def late(step, carry):
+        spread(step, 14)
         fetch(step + 1)
-        spread(step)
-        group, chip = chip_at(place, step)
-        tell(group, chip * 2)
-        tell(group, chip * 2 + 1)
         return carry
 
-    lax.fori_loop(1, 64, early, 0)
-
-    def late(step, carry):
-        fetch(step + 1)
-        spread(step)
-        return carry
-
+    finish(first, HELD * 32, 12)
     lax.fori_loop(64, 126, late, 0)
-    spread(126)
+    spread(126, 14)
     gather_first(first, mine * 32, mine)
     notes[pl.ds(mine, 1)] = note_out[pl.ds(mine, 1)]
 
     local[3].wait()
     local[4].wait()
     local[5].wait()
+    local[8].wait()
+    z_here[...] = jnp.sqrt(bulk[...] * dens[...]).reshape(1, 1, 128)
+    z_all[pl.ds(mine, 1)] = z_here[...]
+
+    def tell_z(step, carry):
+        group, chip = chip_at(place, step // 2)
+        copy(z_here, z_all.at[pl.ds(mine, 1)], 5, group, chip * 2 + (core + step) % 2)
+        return carry
+
+    lax.fori_loop(1, 128, tell_z, 0)
+    ask_in[...] = jnp.zeros((384, 1, 128), jnp.float32)
     prepare(
-        mine, near[...], turn[...], wall[...], bulk[...], dens[...], stack, moves, kept
+        mine, near[...], turn[...], wall[...], bulk[...], dens[...], inside[2, :32, :], stack,
+        moves, kept,
     )
-    ask[...] = jnp.zeros((256, 1, 128), jnp.float32)
     finish(notes, 127, 1)
     note = notes.reshape(128, 128)[...]
     lane = lax.broadcasted_iota(jnp.int32, (128, 128), 1)
@@ -382,11 +428,14 @@
             )
         )
     perm[...] = jnp.concatenate(rows, axis=0).T.astype(jnp.bfloat16)
-    facing[...] = note.astype(jnp.float32).T
+    facing = note.astype(jnp.float32).T
+    for face in range(6):
+        to = facing[8 + face : 9 + face, :] - 1.0
+        chosen = jnp.where(to == sub.astype(jnp.float32), 1.0, 0.0).astype(jnp.bfloat16)
+        moves[ROUTE + face // 2, pl.ds(128 * (1 - face % 2), 128)] = chosen
     local[7].wait()
-    local[8].wait()
     to_index.wait()
-    finish(first, 127 * 32, 3)
+    finish(first, 127 * 32, 16 + core)
 
     def gather_second(target, base, at):
         found = [first[pl.ds(index[j, at], 1)] for j in range(16)]
@@ -424,46 +473,39 @@
     sign = jnp.where(low, -1.0, 1.0)
     z_in = kept[Z_IN]
 
-    def pair(axis, which):
-        if axis == 0:
-            return jnp.where(low, field[which], field[12 + which])
-        found = pick_lanes(field[which], fixed[TAKE + 4 * (axis - 1)])
-        for q in range(1, 4):
-            found = found + pick_lanes(field[4 * q + which], fixed[TAKE + 4 * (axis - 1) + q])
-        return found
-
-    ask_rows = ask.reshape(256, 128)
+    def four(which):
+        return jnp.concatenate([field[4 * q + which] for q in range(4)], axis=1)
+
+    def taken(which, axes):
+        table = [
+            jnp.concatenate([fixed[TAKE + 4 * (axis - 1) + q] for q in range(4)], axis=0)
+            for axis in axes
+        ]
+        return pick_lanes(four(which), jnp.concatenate(table, axis=1))
+
+    both = taken(0, (1, 2))
+    pressures = [jnp.where(low, field[0], field[12]), both[:, :128], both[:, 128:]]
+    normals = [jnp.where(low, field[1], field[13]), taken(2, (1,)), taken(3, (2,))]
+    ask_rows = ask.reshape(96, 128)
     for axis in range(3):
-        pressure = pair(axis, 0)
-        normal = sign * pair(axis, 1 + axis)
-        traces[6 + 2 * axis] = pressure
-        traces[7 + 2 * axis] = normal
-        turned = pltpu.roll(pressure + z_in * normal, 64, 1)
-        traces[2 * axis] = jnp.where(low, z_in, turned)
-        traces[2 * axis + 1] = jnp.where(low, turned, z_in)
-        for face in (2 * axis, 2 * axis + 1):
-            if face < 4:
-                ask_rows[pl.ds(64 * face, 32, stride=2), :] = pick_rows(
-                    moves[GIVE + face][:32], traces[face]
-                )
-            else:
-                ask_rows[pl.ds(128 * (face - 4) + 1, 16, stride=8), :] = pick_rows(
-                    moves[GIVE + face][:16], traces[face]
-                )
-
-    def swap(source, target, phase):
-        for step in STEPS:
-            group, member = device_at(step)
-            copy(
-                source.at[pl.ds((group * 32 + member) * 2, 2)],
-                target.at[pl.ds(mine * 2, 2)],
-                phase,
-                group,
-                member,
-            )
-        target[pl.ds(mine * 2, 2)] = source[pl.ds(mine * 2, 2)]
-
-    swap(ask, ask_in, 3)
+        normal = sign * normals[axis]
+        traces[3 + axis] = pressures[axis]
+        traces[6 + axis] = normal
+        turned = pltpu.roll(pressures[axis] + z_in * normal, 64, 1)
+        traces[axis] = turned
+        found = pick_rows(moves[GIVE + axis, :64], turned)
+        ask_rows[pl.ds(axis, 32, stride=3), :] = jnp.where(low[:32], found[:32], found[32:])
+
+    def three(step, number, source, target, phase):
+        group, member = device_at(step)
+        at = group * 32 + member if number is None else number
+        copy(
+            source.at[pl.ds(at * 3, 3)], target.at[pl.ds(mine * 3, 3)], phase, group, member
+        )
+
+    for number in range(31, 0, -1):
+        three(NEARBY[number], number, ask, ask_in, 3)
+    ask_in[pl.ds(mine * 3, 3)] = ask[pl.ds(0, 3)]
 
     scale = jnp.float32(-metric_scale) * kept[BULK]
     thin = jnp.float32(-metric_scale) * kept[THIN]
@@ -486,86 +528,105 @@
     side_x = along_x(1)
     grad_x = along_x(0)
     for q in range(4):
-        side = side_x[q] + exact(field[4 * q + 2], inside[0])
-        side = side + exact(field[4 * q + 3], inside[1])
-        total[4 * q] = scale * side
+        total[4 * q] = side_x[q]
         total[4 * q + 1] = thin * grad_x[q]
-        total[4 * q + 2] = thin * exact(field[4 * q], inside[0])
-        total[4 * q + 3] = thin * exact(field[4 * q], inside[1])
-
-    finish(ask_in, 254, 7)
-    asked = ask_in.reshape(256, 128)
-    answer_rows = answer.reshape(256, 128)
-    sub_f = sub.astype(jnp.float32)
-    for spot in range(2):
-        face = mine // 32 if spot == 0 else 4 + mine // 64
-        to = facing[pl.ds(8 + face, 1), :] - 1.0
-        chosen = jnp.where(to == sub_f, 1.0, 0.0).astype(jnp.bfloat16)
-        answer_rows[pl.ds(spot, 128, stride=2), :] = pick_rows(
-            chosen, asked[pl.ds(spot, 128, stride=2), :]
-        )
-    swap(answer, answer_in, 4)
-
-    outside = [pick_rows(moves[NEAR + face], traces[face ^ 1]) for face in range(6)]
-
-    finish(answer_in, 254, 9)
-    answers = answer_in.reshape(256, 128)
-    for face in range(6):
-        if face < 4:
-            brought = answers[pl.ds(64 * (face ^ 1), 32, stride=2), :]
-            picked = pick_rows(moves[FAR + face][:, :32], brought)
-        else:
-            brought = answers[pl.ds(128 * ((face ^ 1) - 4) + 1, 16, stride=8), :]
-            picked = pick_rows(moves[FAR + face][:, :16], brought)
-        outside[face] = outside[face] + picked
+
+    finish(ask_in, 93, 7)
+    asked = ask_in.reshape(384, 128)
+    answer_rows = answer.reshape(384, 128)
+    for axis in range(3):
+        found = pick_rows(moves[ROUTE + axis], asked[pl.ds(axis, 128, stride=3), :])
+        answer_rows[pl.ds(axis, 128, stride=3), :] = jnp.where(low, found[:128], found[128:])
+    for step in STEPS:
+        three(step, None, answer, answer_in, 4)
+    answer_in[pl.ds(mine * 3, 3)] = answer[pl.ds(mine * 3, 3)]
+
+    finish(z_all, 127, 11)
+    z_table = z_all.reshape(128, 128)[...]
+    lane_f = lane.astype(jnp.float32)
+    for axis in range(3):
+        found = pick_rows(moves[OWNER + axis], z_table)
+        sides = []
+        for half in range(2):
+            spot = kept[SPOT + axis, :, 64 * half : 64 * half + 1]
+            sides.append(
+                jnp.sum(
+                    jnp.where(lane_f == spot, found[128 * half : 128 * half + 128], 0.0),
+                    axis=1,
+                    keepdims=True,
+                )
+            )
+        kept[SPOT + axis] = jnp.where(low, sides[0], sides[1])
+        found = pick_rows(moves[NEAR + axis], traces[axis])
+        traces[axis] = jnp.where(low, found[:128], found[128:])
+
+    def stacked(which):
+        return jnp.concatenate([field[4 * q + which] for q in range(4)], axis=0)
+
+    side_y = exact(stacked(2), inside[0])
+    side_z = exact(stacked(3), inside[1])
+    grad_y = exact(stacked(0), inside[0])
+    grad_z = exact(stacked(0), inside[1])
+    for q in range(4):
+        rows = slice(128 * q, 128 * q + 128)
+        total[4 * q] = scale * (total[4 * q] + side_y[rows] + side_z[rows])
+        total[4 * q + 2] = thin * grad_y[rows]
+        total[4 * q + 3] = thin * grad_z[rows]
+
+    finish(answer_in, 381, 9)
+    answers = answer_in.reshape(384, 128)
+    coming = []
+    for axis in range(3):
+        found = pick_rows(moves[FAR + axis], answers[pl.ds(axis, 128, stride=3), :])
+        coming.append(traces[axis] + jnp.where(low, found[:128], found[128:]))
+    coming = jnp.concatenate(coming, axis=0)
+    code = jnp.concatenate([kept[CODE + axis] for axis in range(3)], axis=0).astype(jnp.int32)
+    coming = jnp.where(code % 2 == 1, pick_lanes(coming, fixed[TURN]), coming)
+    coming = jnp.where(code // 2 % 2 == 1, pick_lanes(coming, fixed[TURN + 1]), coming)
+    coming = jnp.where(code >= 4, pick_lanes(coming, fixed[TURN + 2]), coming)
     lift = jnp.float32(metric_scale / float(gll_tables(NP - 1)[1][0]))
     gains = []
     for axis in range(3):
-        even, odd = outside[2 * axis], outside[2 * axis + 1]
-        coming = jnp.where(low, even, odd)
-        z_out = pltpu.roll(jnp.where(low, odd, even), 64, 1)
-        code = kept[CODE + axis].astype(jnp.int32)
-        coming = jnp.where(code % 2 == 1, pick_lanes(coming, fixed[TURN]), coming)
-        coming = jnp.where(code // 2 % 2 == 1, pick_lanes(coming, fixed[TURN + 1]), coming)
-        coming = jnp.where(code >= 4, pick_lanes(coming, fixed[TURN + 2]), coming)
         is_wall = kept[WALL + axis] == 1.0
-        pressure = traces[6 + 2 * axis]
-        normal = traces[7 + 2 * axis]
-        z_out = jnp.where(is_wall, z_in, z_out)
-        jump = jnp.where(is_wall, 2.0 * z_in * normal, coming - pressure + z_out * normal)
+        normal = traces[6 + axis]
+        z_out = jnp.where(is_wall, z_in, kept[SPOT + axis])
+        other = coming[128 * axis : 128 * axis + 128]
+        jump = jnp.where(
+            is_wall, 2.0 * z_in * normal, other - traces[3 + axis] + z_out * normal
+        )
         jump = lift * jump / (z_in + z_out)
         gains.append(jnp.concatenate([kept[BULK] * jump, -sign * kept[THIN] * z_in * jump]))
+    lifted = []
+    for axis in (1, 2):
+        wide = jnp.concatenate([fixed[LIFT + 4 * (axis - 1) + q] for q in range(4)], axis=1)
+        lifted.append(pick_lanes(gains[axis], wide))
     for q in range(4):
-        if q == 0:
-            along = jnp.where(jnp.concatenate([low, low]), gains[0], 0.0)
-        elif q == 3:
-            along = jnp.where(jnp.concatenate([low, low]), 0.0, gains[0])
-        else:
-            along = None
-        lifted = [along] + [
-            pick_lanes(gains[axis], fixed[LIFT + 4 * (axis - 1) + q]) for axis in (1, 2)
-        ]
-        part = total[4 * q] + lifted[1][:128] + lifted[2][:128]
+        lanes = slice(128 * q, 128 * q + 128)
+        part = total[4 * q] + lifted[0][:128, lanes] + lifted[1][:128, lanes]
         part_x = total[4 * q + 1]
-        if along is not None:
-            part = part + along[:128]
-            part_x = part_x + along[128:]
+        if q in (0, 3):
+            keep = low if q == 0 else lane >= 64
+            part = part + jnp.where(keep, gains[0][:128], 0.0)
+            part_x = part_x + jnp.where(keep, gains[0][128:], 0.0)
         out_ref[pl.ds(4 * q, 128, stride=16), :] = part
         out_ref[pl.ds(4 * q + 1, 128, stride=16), :] = part_x
-        out_ref[pl.ds(4 * q + 2, 128, stride=16), :] = total[4 * q + 2] + lifted[1][128:]
-        out_ref[pl.ds(4 * q + 3, 128, stride=16), :] = total[4 * q + 3] + lifted[2][128:]
+        out_ref[pl.ds(4 * q + 2, 128, stride=16), :] = total[4 * q + 2] + lifted[0][128:, lanes]
+        out_ref[pl.ds(4 * q + 3, 128, stride=16), :] = total[4 * q + 3] + lifted[1][128:, lanes]
     finish(notes, 127, 0)
-    finish(first, 127 * 32, 2)
+    finish(first, 32, 2)
+    finish(first, (63 - HELD) * 32, 13)
+    finish(first, 63 * 32, 14)
+    finish(z_all, 127, 10)
     finish(third, 127 * 16, 4)
-    finish(ask_in, 254, 6)
-    finish(answer_in, 254, 8)
+    finish(ask_in, 93, 6)
+    finish(answer_in, 381, 8)
 
 
 def body(old_state, dest_row, neighbours, orientation, wall_flags, bulk_modulus, density):
     view = old_state.reshape(256, 4, 4, 128).transpose(0, 2, 1, 3).reshape(4096, 1, 128)
     picks, inside = fixed_tables()
     f32, i32, bf16 = jnp.float32, jnp.int32, jnp.bfloat16
-    halo = pltpu.VMEM((256, 1, 128), f32)
+    halo = pltpu.VMEM((384, 1, 128), f32)
     result = pl.pallas_call(
         exchange_kernel,
         out_shape=jax.ShapeDtypeStruct((2048, 128), f32),
@@ -580,7 +641,7 @@
             pltpu.VMEM((1, 128), f32),
             pltpu.VMEM((1, 128), f32),
             pltpu.VMEM((19, 128, 128), bf16),
-            pltpu.VMEM((2, 128, 128), f32),
+            pltpu.VMEM((3, 128, 128), f32),
             pltpu.VMEM((2, 128), i32),
             pltpu.SMEM((2, 128), i32),
             pltpu.VMEM((128, 1, 128), i32),
@@ -593,17 +654,18 @@
             pltpu.SMEM((16, 128), i32),
             pltpu.VMEM((128, 128), bf16),
             pltpu.VMEM((128, 128), f32),
-            pltpu.VMEM((128, 128), f32),
-            pltpu.VMEM((18, 128, 128), bf16),
+            pltpu.VMEM((1, 1, 128), f32),
+            pltpu.VMEM((128, 1, 128), f32),
+            pltpu.VMEM((15, 256, 128), bf16),
             pltpu.VMEM((KEPT, 128, 128), f32),
             pltpu.VMEM((16, 128, 128), f32),
-            pltpu.VMEM((12, 128, 128), f32),
-            halo,
+            pltpu.VMEM((9, 128, 128), f32),
+            pltpu.VMEM((96, 1, 128), f32),
             halo,
             halo,
             halo,
             pltpu.VMEM((16, 128, 128), f32),
-            pltpu.SemaphoreType.DMA((10,)),
+            pltpu.SemaphoreType.DMA((18,)),
             pltpu.SemaphoreType.DMA((11,)),
             pltpu.SemaphoreType.REGULAR,
             pltpu.SemaphoreType.REGULAR,

time: 73.3 us -> 73.2 us (level)
  no operation moved by 1% of the time
where the time goes in v4:
time: 73.2 us; the launch traced here: 73.1 us
  Pallas kernels  70.8 us (97%)
  local copies, waits for them, and re-layouts  2.26 us (3%)
    pallas_call x1, Pallas kernels, body(): pl.pallas_call(exchange_kernel, out_shape=jax.ShapeDtypeStruct((2048, 128...  70.8 us
    unnamed x1, local copies, waits for them, and re-layouts  2.26 us

profile of v4, /device:TPU:1, one launch (start us, length us, event | category | flops | bytes accessed | tf_op | source)
XLA Modules:
  0.0 73.1 jit_solution(6544184116230620966)
XLA Ops:
  0.0 70.8 %shard_map.91 = f32[2048,128]{1,0:T(8,128)} custom-call(f32[4096,1,128]{2,1,0:T(1,128)} %bitcast.14, s32[2,128]{1,0:T(2,128)} %bitcast.15, s32[6,128]{1,0:T(8,128)} %near_ref.1, s32[6,128]{1,0:T(8,128)} %turn_ref.1, s32[6,128]{1,0:T(8,128)} %wall_ref.1, f32[1,128]{1,0:T(1,128)} %bitcast.16, f32[1,128]{1,0:T(1,128)} %bitcast.17, ...), custom_call_target="tpu_custom_call" | custom-call | tf_op jit(solution)/shard_map/pallas_call | solution.py:630
  70.8 2.3 %copy.13 = f32[128,4,512]{2,1,0:T(4,128)} copy(f32[128,4,512]{2,1,0:T(4,128)} %bitcast.13) | data formatting | bytes 2097152

commit v5 on v4

--- a/solution.py
+++ b/solution.py
@@ -9,7 +9,6 @@
 NP = 8
 MESH = pl.DeviceIdType.MESH
 HIGHEST = lax.Precision.HIGHEST
-HELD = 48
 
 metric_scale = 0.25
 
@@ -357,30 +356,20 @@
     spread(0, 2)
     tell(z_at, member_here + 1 - 2 * core)
 
-    def early(leaves):
-        def one(step, carry):
-            fetch(step + 1)
-            spread(step, leaves)
-            group, chip = chip_at(place, step)
-            tell(group, chip * 2)
-            tell(group, chip * 2 + 1)
-            return carry
-
-        return one
-
-    lax.fori_loop(1, HELD + 1, early(12), 0)
-    lax.fori_loop(HELD + 1, 64, early(13), 0)
+    def early(step, carry):
+        fetch(step + 1)
+        spread(step, 12)
+        group, chip = chip_at(place, step)
+        tell(group, chip * 2)
+        tell(group, chip * 2 + 1)
+        return carry
+
+    lax.fori_loop(1, 64, early, 0)
 
     def late(step, carry):
         spread(step, 14)
         fetch(step + 1)
         return carry
-
-    finish(first, HELD * 32, 12)
-    lax.fori_loop(64, 126, late, 0)
-    spread(126, 14)
-    gather_first(first, mine * 32, mine)
-    notes[pl.ds(mine, 1)] = note_out[pl.ds(mine, 1)]
 
     local[3].wait()
     local[4].wait()
@@ -389,17 +378,13 @@
     z_here[...] = jnp.sqrt(bulk[...] * dens[...]).reshape(1, 1, 128)
     z_all[pl.ds(mine, 1)] = z_here[...]
 
-    def tell_z(step, carry):
-        group, chip = chip_at(place, step // 2)
-        copy(z_here, z_all.at[pl.ds(mine, 1)], 5, group, chip * 2 + (core + step) % 2)
-        return carry
-
-    lax.fori_loop(1, 128, tell_z, 0)
     ask_in[...] = jnp.zeros((384, 1, 128), jnp.float32)
-    prepare(
-        mine, near[...], turn[...], wall[...], bulk[...], dens[...], inside[2, :32, :], stack,
-        moves, kept,
-    )
+    finish(first, 63 * 32, 12)
+    lax.fori_loop(64, 126, late, 0)
+    spread(126, 14)
+    gather_first(first, mine * 32, mine)
+    notes[pl.ds(mine, 1)] = note_out[pl.ds(mine, 1)]
+
     finish(notes, 127, 1)
     note = notes.reshape(128, 128)[...]
     lane = lax.broadcasted_iota(jnp.int32, (128, 128), 1)
@@ -463,6 +448,17 @@
         before = (group, member)
     gather_second(third, mine * 16, mine)
     forward(*before)
+
+    def tell_z(step, carry):
+        group, chip = chip_at(place, step // 2)
+        copy(z_here, z_all.at[pl.ds(mine, 1)], 5, group, chip * 2 + (core + step) % 2)
+        return carry
+
+    lax.fori_loop(1, 128, tell_z, 0)
+    prepare(
+        mine, near[...], turn[...], wall[...], bulk[...], dens[...], inside[2, :32, :], stack,
+        moves, kept,
+    )
     finish(third, 127 * 16, 5)
 
     arrived = third.reshape(8, 16, 16, 128)
@@ -614,7 +610,6 @@
         out_ref[pl.ds(4 * q + 3, 128, stride=16), :] = total[4 * q + 3] + lifted[1][128:, lanes]
     finish(notes, 127, 0)
     finish(first, 32, 2)
-    finish(first, (63 - HELD) * 32, 13)
     finish(first, 63 * 32, 14)
     finish(z_all, 127, 10)
     finish(third, 127 * 16, 4)

time: 73.2 us -> 69.4 us (0.948)
  Pallas kernels: 70.8 us -> 67 us
    pallas_call x1, Pallas kernels: 70.8 us -> 67 us  [body(): pl.pallas_call(exchange_kernel, out_shape=jax.ShapeDtypeStruct((2048, 128...]
where the time goes in v5:
time: 69.4 us; the launch traced here: 69.3 us
  Pallas kernels  67 us (97%)
  local copies, waits for them, and re-layouts  2.26 us (3%)
    pallas_call x1, Pallas kernels, body(): pl.pallas_call(exchange_kernel, out_shape=jax.ShapeDtypeStruct((2048, 128...  67 us
    unnamed x1, local copies, waits for them, and re-layouts  2.26 us

profile of v5, /device:TPU:1, one launch (start us, length us, event | category | flops | bytes accessed | tf_op | source)
XLA Modules:
  0.0 69.3 jit_solution(13805950359121169680)
XLA Ops:
  0.0 67.0 %shard_map.91 = f32[2048,128]{1,0:T(8,128)} custom-call(f32[4096,1,128]{2,1,0:T(1,128)} %bitcast.14, s32[2,128]{1,0:T(2,128)} %bitcast.15, s32[6,128]{1,0:T(8,128)} %near_ref.1, s32[6,128]{1,0:T(8,128)} %turn_ref.1, s32[6,128]{1,0:T(8,128)} %wall_ref.1, f32[1,128]{1,0:T(1,128)} %bitcast.16, f32[1,128]{1,0:T(1,128)} %bitcast.17, ...), custom_call_target="tpu_custom_call" | custom-call | tf_op jit(solution)/shard_map/pallas_call | solution.py:625
  67.0 2.3 %copy.13 = f32[128,4,512]{2,1,0:T(4,128)} copy(f32[128,4,512]{2,1,0:T(4,128)} %bitcast.13) | data formatting | bytes 2097152

commit v6 on v5

--- a/solution.py
+++ b/solution.py
@@ -92,9 +92,10 @@
 
 def chip_at(place, step):
     z_at, y_at, x_at, _ = place
+    step = step * 37 % 64
     x_to = (x_at + step) % 4
-    y_to = (y_at + step // 4 + step) % 4
-    z_to = (z_at + step // 16 + step // 4 + step) % 4
+    y_to = (y_at + step // 4) % 4
+    z_to = (z_at + step // 16) % 4
     return z_to, y_to * 4 + x_to
 
 
@@ -364,7 +365,7 @@
         tell(group, chip * 2 + 1)
         return carry
 
-    lax.fori_loop(1, 64, early, 0)
+    lax.fori_loop(1, 64, early, 0, unroll=3)
 
     def late(step, carry):
         spread(step, 14)
@@ -380,7 +381,7 @@
 
     ask_in[...] = jnp.zeros((384, 1, 128), jnp.float32)
     finish(first, 63 * 32, 12)
-    lax.fori_loop(64, 126, late, 0)
+    lax.fori_loop(64, 126, late, 0, unroll=2)
     spread(126, 14)
     gather_first(first, mine * 32, mine)
     notes[pl.ds(mine, 1)] = note_out[pl.ds(mine, 1)]
@@ -449,12 +450,8 @@
     gather_second(third, mine * 16, mine)
     forward(*before)
 
-    def tell_z(step, carry):
-        group, chip = chip_at(place, step // 2)
-        copy(z_here, z_all.at[pl.ds(mine, 1)], 5, group, chip * 2 + (core + step) % 2)
-        return carry
-
-    lax.fori_loop(1, 128, tell_z, 0)
+    for step in STEPS:
+        copy(z_here, z_all.at[pl.ds(mine, 1)], 5, *device_at(step))
     prepare(
         mine, near[...], turn[...], wall[...], bulk[...], dens[...], inside[2, :32, :], stack,
         moves, kept,
@@ -520,12 +517,6 @@
                 found = term if found is None else found + term
             sums.append(found)
         return sums
-
-    side_x = along_x(1)
-    grad_x = along_x(0)
-    for q in range(4):
-        total[4 * q] = side_x[q]
-        total[4 * q + 1] = thin * grad_x[q]
 
     finish(ask_in, 93, 7)
     asked = ask_in.reshape(384, 128)
@@ -558,6 +549,12 @@
 
     def stacked(which):
         return jnp.concatenate([field[4 * q + which] for q in range(4)], axis=0)
+
+    side_x = along_x(1)
+    grad_x = along_x(0)
+    for q in range(4):
+        total[4 * q] = side_x[q]
+        total[4 * q + 1] = thin * grad_x[q]
 
     side_y = exact(stacked(2), inside[0])
     side_z = exact(stacked(3), inside[1])
@@ -615,6 +612,17 @@
     finish(third, 127 * 16, 4)
     finish(ask_in, 93, 6)
     finish(answer_in, 381, 8)
+
+
+def write_kernel(in_ref, out_ref, rows, sems):
+    parts = [pl.ds(512 * n, 512) for n in range(4)]
+    for n, part in enumerate(parts):
+        pltpu.make_async_copy(in_ref.at[part], rows.at[part], sems.at[n]).start()
+    for n, part in enumerate(parts):
+        pltpu.make_async_copy(in_ref.at[part], rows.at[part], sems.at[n]).wait()
+        pltpu.make_async_copy(rows.at[part], out_ref.at[part], sems.at[4 + n]).start()
+    for n, part in enumerate(parts):
+        pltpu.make_async_copy(rows.at[part], out_ref.at[part], sems.at[4 + n]).wait()
 
 
 def body(old_state, dest_row, neighbours, orientation, wall_flags, bulk_modulus, density):
@@ -677,6 +685,13 @@
         jnp.asarray(picks, bf16),
         jnp.asarray(inside),
     )
+    result = pl.pallas_call(
+        write_kernel,
+        out_shape=jax.ShapeDtypeStruct((2048, 128), f32),
+        in_specs=[pl.BlockSpec(memory_space=pl.ANY)],
+        out_specs=pl.BlockSpec(memory_space=pl.ANY),
+        scratch_shapes=[pltpu.VMEM((2048, 128), f32), pltpu.SemaphoreType.DMA((8,))],
+    )(result)
     return result.reshape(128, 4, 4, 128).transpose(0, 2, 1, 3).reshape(128, 4, 512)
 
 

time: 69.4 us -> 68.5 us (0.987)
  local copies, waits for them, and re-layouts: 2.26 us -> 0 us
  Pallas kernels: 67 us -> 68.4 us
    unnamed x1 -> x0, local copies, waits for them, and re-layouts: 2.26 us -> none
    pallas_call x0 -> x1, Pallas kernels: none -> 1.98 us  [body(): pl.pallas_call(write_kernel, out_shape=jax.ShapeDtypeStruct((2048, 128),...]
where the time goes in v6:
time: 68.5 us; the launch traced here: 68.4 us
  Pallas kernels  68.4 us (100%)
    pallas_call x1, Pallas kernels, body(): pl.pallas_call(exchange_kernel, out_shape=jax.ShapeDtypeStruct((2048, 128...  66.4 us
    pallas_call x1, Pallas kernels, body(): pl.pallas_call(write_kernel, out_shape=jax.ShapeDtypeStruct((2048, 128),...  1.98 us

profile of v6, /device:TPU:1, one launch (start us, length us, event | category | flops | bytes accessed | tf_op | source)
XLA Modules:
  0.0 68.4 jit_solution(11020455295917959794)
XLA Ops:
  0.0 66.4 %shard_map.91.in_ref = f32[2048,128]{1,0:T(8,128)} custom-call(f32[4096,1,128]{2,1,0:T(1,128)} %bitcast.13, s32[2,128]{1,0:T(2,128)} %bitcast.14, s32[6,128]{1,0:T(8,128)} %near_ref.1, s32[6,128]{1,0:T(8,128)} %turn_ref.1, s32[6,128]{1,0:T(8,128)} %wall_ref.1, f32[1,128]{1,0:T(1,128)} %bitcast.15, f32[1,128]{1,0:T(1,128)} %bitcast.16, ...), custom_call_target="tpu_custom_call" | custom-call | tf_op jit(solution)/shard_map/pallas_call | solution.py:633
  66.4 2.0 %shard_map.92 = f32[2048,128]{1,0:T(8,128)} custom-call(f32[2048,128]{1,0:T(8,128)} %shard_map.91.in_ref), custom_call_target="tpu_custom_call" | custom-call | tf_op jit(solution)/shard_map/pallas_call | solution.py:688

commit v7 on v6

--- a/solution.py
+++ b/solution.py
@@ -92,7 +92,7 @@
 
 def chip_at(place, step):
     z_at, y_at, x_at, _ = place
-    step = step * 37 % 64
+    step = step * 27 % 64
     x_to = (x_at + step) % 4
     y_to = (y_at + step // 4) % 4
     z_to = (z_at + step // 16) % 4

time: 68.5 us -> 68.2 us (level)
  no operation moved by 1% of the time
where the time goes in v7:
time: 68.2 us; the launch traced here: 68.1 us
  Pallas kernels  68.1 us (100%)
    pallas_call x1, Pallas kernels, body(): pl.pallas_call(exchange_kernel, out_shape=jax.ShapeDtypeStruct((2048, 128...  66.1 us
    pallas_call x1, Pallas kernels, body(): pl.pallas_call(write_kernel, out_shape=jax.ShapeDtypeStruct((2048, 128),...  1.98 us

profile of v7, /device:TPU:1, one launch (start us, length us, event | category | flops | bytes accessed | tf_op | source)
XLA Modules:
  0.0 68.1 jit_solution(17465447002402135000)
XLA Ops:
  0.0 66.1 %shard_map.91.in_ref = f32[2048,128]{1,0:T(8,128)} custom-call(f32[4096,1,128]{2,1,0:T(1,128)} %bitcast.13, s32[2,128]{1,0:T(2,128)} %bitcast.14, s32[6,128]{1,0:T(8,128)} %near_ref.1, s32[6,128]{1,0:T(8,128)} %turn_ref.1, s32[6,128]{1,0:T(8,128)} %wall_ref.1, f32[1,128]{1,0:T(1,128)} %bitcast.15, f32[1,128]{1,0:T(1,128)} %bitcast.16, ...), custom_call_target="tpu_custom_call" | custom-call | tf_op jit(solution)/shard_map/pallas_call | solution.py:633
  66.1 2.0 %shard_map.92 = f32[2048,128]{1,0:T(8,128)} custom-call(f32[2048,128]{1,0:T(8,128)} %shard_map.91.in_ref), custom_call_target="tpu_custom_call" | custom-call | tf_op jit(solution)/shard_map/pallas_call | solution.py:688

commit v8 on v7

--- a/solution.py
+++ b/solution.py
@@ -572,11 +572,16 @@
     for axis in range(3):
         found = pick_rows(moves[FAR + axis], answers[pl.ds(axis, 128, stride=3), :])
         coming.append(traces[axis] + jnp.where(low, found[:128], found[128:]))
-    coming = jnp.concatenate(coming, axis=0)
-    code = jnp.concatenate([kept[CODE + axis] for axis in range(3)], axis=0).astype(jnp.int32)
-    coming = jnp.where(code % 2 == 1, pick_lanes(coming, fixed[TURN]), coming)
-    coming = jnp.where(code // 2 % 2 == 1, pick_lanes(coming, fixed[TURN + 1]), coming)
-    coming = jnp.where(code >= 4, pick_lanes(coming, fixed[TURN + 2]), coming)
+    parts = jnp.concatenate(
+        [part.astype(jnp.float32) for part in split3(jnp.concatenate(coming, axis=0))], axis=0
+    )
+    code = jnp.concatenate([kept[CODE + axis] for axis in range(3)] * 3, axis=0).astype(jnp.int32)
+    for number, turns in enumerate((code % 2 == 1, code // 2 % 2 == 1, code >= 4)):
+        found = jnp.dot(
+            parts.astype(jnp.bfloat16), fixed[TURN + number], preferred_element_type=jnp.float32
+        )
+        parts = jnp.where(turns, found, parts)
+    coming = parts[:384] + parts[384:768] + parts[768:]
     lift = jnp.float32(metric_scale / float(gll_tables(NP - 1)[1][0]))
     gains = []
     for axis in range(3):

time: 68.2 us -> 68 us (level)
  no operation moved by 1% of the time
where the time goes in v8:
time: 68 us; the launch traced here: 67.8 us
  Pallas kernels  67.8 us (100%)
    pallas_call x1, Pallas kernels, body(): pl.pallas_call(exchange_kernel, out_shape=jax.ShapeDtypeStruct((2048, 128...  65.9 us
    pallas_call x1, Pallas kernels, body(): pl.pallas_call(write_kernel, out_shape=jax.ShapeDtypeStruct((2048, 128),...  1.98 us

profile of v8, /device:TPU:1, one launch (start us, length us, event | category | flops | bytes accessed | tf_op | source)
XLA Modules:
  0.0 67.8 jit_solution(10833680094091079150)
XLA Ops:
  0.0 65.9 %shard_map.91.in_ref = f32[2048,128]{1,0:T(8,128)} custom-call(f32[4096,1,128]{2,1,0:T(1,128)} %bitcast.13, s32[2,128]{1,0:T(2,128)} %bitcast.14, s32[6,128]{1,0:T(8,128)} %near_ref.1, s32[6,128]{1,0:T(8,128)} %turn_ref.1, s32[6,128]{1,0:T(8,128)} %wall_ref.1, f32[1,128]{1,0:T(1,128)} %bitcast.15, f32[1,128]{1,0:T(1,128)} %bitcast.16, ...), custom_call_target="tpu_custom_call" | custom-call | tf_op jit(solution)/shard_map/pallas_call | solution.py:638
  65.9 2.0 %shard_map.92 = f32[2048,128]{1,0:T(8,128)} custom-call(f32[2048,128]{1,0:T(8,128)} %shard_map.91.in_ref), custom_call_target="tpu_custom_call" | custom-call | tf_op jit(solution)/shard_map/pallas_call | solution.py:693
